TPU v7x, 512 devices: a whole 4x8x8 slice. The times are simulated.
512 devices in a mesh: fsdp: 64 (over z, y), rep: 8 (over x, core).
Axes of the slice: x: 4, y: 8, z: 8, core: 2. Of those that a mesh axis runs over, the one named last changes fastest.
Arguments:
- params: float32 [24576, 3584], P(('fsdp', 'rep')), may hold values from -6 to 6
- grads: bfloat16 [24576, 3584], P(('fsdp', 'rep')), may hold values from -6 to 6
- moments: bfloat16 [3, 24576, 3584], P(None, ('fsdp', 'rep')), may hold values from -6 to 6
- row_acc: float32 [24576], P(('fsdp', 'rep')), may hold values from 0.05 to 1
- lengths: int32 [128], replicated, may hold values from 1 to 384, 24576 in all
- tensor_order: int32 [128], replicated, may hold values from 0 to 127, each once
- col_acc: float32 [128, 3584], P('fsdp'), may hold values from 0.05 to 1
- hidden_state: float32 [128, 512], P('fsdp'), may hold values from -1 to 1
- cell_state: float32 [128, 512], P('fsdp'), may hold values from -4 to 4
- lstm_in: bfloat16 [10, 2048], replicated, may hold values from -2 to 2
- lstm_rec: bfloat16 [512, 2048], replicated, may hold values from -0.25 to 0.25
- lstm_bias: float32 [2048], replicated, may hold values from -3 to 3
- hyper_first: bfloat16 [512, 256], replicated, may hold values from -0.25 to 0.25
- hyper_rest: bfloat16 [512, 128], replicated, may hold values from -0.25 to 0.25
Outputs:
- update: float32 [24576, 3584], P(('fsdp', 'rep'))
- row_new: float32 [24576], P(('fsdp', 'rep'))
- col_new: float32 [128, 3584], P('fsdp')
- hidden_new: float32 [128, 512], P('fsdp')
- cell_new: float32 [128, 512], P('fsdp')
Inputs may be any that keep to these rules, and one draw needn't show every extreme that they name: `lengths`: they sum to 24576; the largest is 384. `tensor_order`: owner slot i belongs to fsdp index i // 2; each tensor appears once.
All inputs are finite; a program needn't handle non-finite values.
Results may differ from a plain program's by a relative error of at most 0.019.
Values may be sent and summed in bfloat16 or wider, within the bound.
A program may use at most 64 MiB of HBM per device.

v0:
```python
import math

import jax
import jax.numpy as jnp
from jax import lax
from jax.sharding import PartitionSpec as P

EPSILON = 1e-06
DECAY_RATE = 0.9


def in_blocks(array, dim, length):
    shape = array.shape
    parts = array.reshape(*shape[:dim], length, shape[dim] // length, *shape[dim + 1 :])
    return jnp.moveaxis(parts, dim, 0)


def sent_and_summed(array, axis, dim):
    parts = in_blocks(array, dim, lax.axis_size(axis))
    arrived = lax.all_to_all(parts, axis, split_axis=0, concat_axis=0, tiled=True)
    return arrived.sum(axis=0)


def sent_together(arrays, axis, dim, along):
    ends, at = ([], 0)
    for a in arrays[:-1]:
        at += a.shape[along]
        ends.append(at)
    both = jnp.concatenate(arrays, axis=along)
    return tuple(jnp.split(sent_and_summed(both, axis, dim), ends, axis=along))


def sent_to_all(array, axis):
    copies = jnp.broadcast_to(array, (lax.axis_size(axis), *array.shape))
    return lax.all_to_all(copies, axis, split_axis=0, concat_axis=0, tiled=True)


def taken_together(array, axis):
    return sent_to_all(array, axis).sum(axis=0)


def together(arrays, axis):
    ravelled, at, gathered = (jnp.concatenate([a.reshape(-1) for a in arrays]), 0, [])
    so_far = taken_together(ravelled, axis)
    for a in arrays:
        gathered.append(so_far[at : at + a.size].reshape(a.shape))
        at += a.size
    return tuple(gathered)


def in_one_piece(arrays, axis, dim, along):
    ends, at = ([], 0)
    for a in arrays[:-1]:
        at += a.shape[along]
        ends.append(at)
    both = jnp.concatenate(arrays, axis=along)
    return tuple(jnp.split(lax.all_gather(both, axis, axis=dim, tiled=True), ends, axis=along))


def owner_step(
    col_sums,
    tensor_stats,
    row_lengths,
    col_acc,
    hidden_state,
    cell_state,
    lstm_in,
    lstm_rec,
    lstm_bias,
    hyper_first,
    hyper_rest,
):
    col_width = col_acc.shape[1]
    col_new = DECAY_RATE * col_acc + (1.0 - DECAY_RATE) * col_sums / row_lengths[:, None]
    tensor_means = tensor_stats / (row_lengths * col_width)[:, None]
    log_means = jnp.log(tensor_means[:, :5] + EPSILON)
    corr_first = tensor_means[:, 5] / jnp.sqrt(tensor_means[:, 0] * tensor_means[:, 1] + EPSILON)
    corr_second = tensor_means[:, 6] / jnp.sqrt(tensor_means[:, 0] * tensor_means[:, 3] + EPSILON)
    corr_third = tensor_means[:, 7] / jnp.sqrt(tensor_means[:, 1] * tensor_means[:, 3] + EPSILON)
    col_mean = jnp.mean(col_new, axis=1)
    col_square = jnp.mean(col_new * col_new, axis=1)
    spread = jnp.log(col_square / (col_mean * col_mean))
    extra = jnp.stack(
        [corr_first, corr_second, corr_third, jnp.log(col_mean + EPSILON), spread], axis=1
    )
    features = jnp.concatenate([log_means, extra], axis=1).astype(jnp.bfloat16)
    gate_sum = jnp.dot(features, lstm_in, preferred_element_type=jnp.float32)
    gate_sum = (
        gate_sum
        + jnp.dot(hidden_state.astype(jnp.bfloat16), lstm_rec, preferred_element_type=jnp.float32)
        + lstm_bias
    )
    hid_width = hidden_state.shape[1]
    gate_in = gate_sum[:, :hid_width]
    gate_forget = gate_sum[:, hid_width : 2 * hid_width]
    gate_cand = gate_sum[:, 2 * hid_width : 3 * hid_width]
    gate_out = gate_sum[:, 3 * hid_width :]
    cell_new = jax.nn.sigmoid(gate_forget) * cell_state + jax.nn.sigmoid(gate_in) * jnp.tanh(
        gate_cand
    )
    hidden_new = jax.nn.sigmoid(gate_out) * jnp.tanh(cell_new)
    hidden_bf = hidden_new.astype(jnp.bfloat16)
    gen_first = jnp.dot(hidden_bf, hyper_first, preferred_element_type=jnp.float32).astype(
        jnp.bfloat16
    )
    gen_rest = jnp.dot(hidden_bf, hyper_rest, preferred_element_type=jnp.float32).astype(
        jnp.bfloat16
    )
    tensor_scales = jnp.stack(
        [
            jnp.sqrt(tensor_means[:, 0] + EPSILON),
            jnp.sqrt(tensor_means[:, 1] + EPSILON),
            jnp.sqrt(tensor_means[:, 4] + EPSILON),
            col_mean,
        ],
        axis=1,
    )
    return (col_new, hidden_new, cell_new, gen_first, gen_rest, tensor_scales)


def param_block(
    param_rows, grad_rows, moment_rows, row_var, col_rows, first_rows, rest_rows, scale_rows
):
    block_rows = param_rows.shape[0]
    grad_f = grad_rows.astype(jnp.float32)
    mom_f = moment_rows.astype(jnp.float32)
    v_factored = row_var[:, None] * col_rows / scale_rows[:, 3:4]
    inv_rms = lax.rsqrt(v_factored + EPSILON)
    grad_norm = grad_f * inv_rms
    mom_norm = mom_f[0] * inv_rms
    inputs = jnp.stack(
        [
            grad_norm,
            mom_norm,
            mom_f[1] * inv_rms,
            mom_f[2] * inv_rms,
            grad_f / scale_rows[:, 0:1],
            mom_f[0] / scale_rows[:, 1:2],
            param_rows / scale_rows[:, 2:3],
            grad_norm * mom_norm,
        ],
        axis=1,
    ).astype(jnp.bfloat16)
    hm_width = rest_rows.shape[1] // 4
    w_first = first_rows.reshape(block_rows, 8, hm_width)
    bias_first = rest_rows[:, :hm_width].astype(jnp.float32)
    w_second = rest_rows[:, hm_width:].reshape(block_rows, hm_width, 3)
    hidden_units = (
        jnp.einsum("bfc,bfh->bhc", inputs, w_first, preferred_element_type=jnp.float32)
        + bias_first[:, :, None]
    )
    hidden_units = jax.nn.relu(hidden_units).astype(jnp.bfloat16)
    mlp_out = jnp.einsum("bhc,bho->boc", hidden_units, w_second, preferred_element_type=jnp.float32)
    return mlp_out[:, 0] * jnp.exp(jnp.tanh(mlp_out[:, 1])) * jax.nn.sigmoid(mlp_out[:, 2])


def on_device(
    params,
    grads,
    moments,
    row_acc,
    lengths,
    tensor_order,
    col_acc,
    hidden_state,
    cell_state,
    lstm_in,
    lstm_rec,
    lstm_bias,
    hyper_first,
    hyper_rest,
):
    row_count = params.shape[0]
    tensor_count = lengths.shape[0]
    own_count = col_acc.shape[0]
    first_row = (lax.axis_index("fsdp") * lax.axis_size("rep") + lax.axis_index("rep")) * row_count
    tensor_ends = jnp.cumsum(lengths)
    global_rows = first_row + lax.iota(jnp.int32, row_count)
    seg_ids = jnp.sum((global_rows[:, None] >= tensor_ends[None, :]).astype(jnp.int32), axis=1)
    row_pick = (seg_ids[:, None] == tensor_order[None, :]).astype(jnp.float32)
    slot_match = tensor_order[:, None] == lax.iota(jnp.int32, tensor_count)[None, :]
    row_lengths = jnp.sum(jnp.where(slot_match, lengths[None, :], 0), axis=1).astype(jnp.float32)
    grad_f = grads.astype(jnp.float32)
    grad_sq = grad_f * grad_f
    row_new = DECAY_RATE * row_acc + (1.0 - DECAY_RATE) * jnp.mean(grad_sq, axis=1)
    mom_zero = moments[0].astype(jnp.float32)
    mom_one = moments[1].astype(jnp.float32)
    mom_two = moments[2].astype(jnp.float32)
    per_row = jnp.stack(
        [
            jnp.sum(grad_sq, axis=1),
            jnp.sum(mom_zero * mom_zero, axis=1),
            jnp.sum(mom_one * mom_one, axis=1),
            jnp.sum(mom_two * mom_two, axis=1),
            jnp.sum(params * params, axis=1),
            jnp.sum(grad_f * mom_zero, axis=1),
            jnp.sum(grad_f * mom_two, axis=1),
            jnp.sum(mom_zero * mom_two, axis=1),
        ],
        axis=1,
    )
    slot_stats = jnp.einsum("ri,rk->ik", row_pick, per_row, precision=lax.Precision.HIGHEST)
    slot_cols = jnp.einsum("ri,rc->ic", row_pick, grad_sq, precision=lax.Precision.HIGHEST)
    mine_start = lax.axis_index("fsdp") * own_count
    col_share, stats_share = sent_together((slot_cols, slot_stats), "fsdp", 0, 1)
    col_part, stats_part = together((col_share, stats_share), "rep")
    my_lengths = lax.dynamic_slice_in_dim(row_lengths, mine_start, own_count, 0)
    col_new, hidden_new, cell_new, gen_first, gen_rest, tensor_scales = owner_step(
        col_part,
        stats_part,
        my_lengths,
        col_acc,
        hidden_state,
        cell_state,
        lstm_in,
        lstm_rec,
        lstm_bias,
        hyper_first,
        hyper_rest,
    )
    col_all, scale_all = in_one_piece((col_new, tensor_scales), "fsdp", 0, 1)
    first_all, rest_all = in_one_piece((gen_first, gen_rest), "fsdp", 0, 1)
    col_rows = jnp.dot(row_pick, col_all, precision=lax.Precision.HIGHEST)
    scale_rows = jnp.dot(row_pick, scale_all, precision=lax.Precision.HIGHEST)
    pick_bf = row_pick.astype(jnp.bfloat16)
    first_rows = jnp.dot(pick_bf, first_all, preferred_element_type=jnp.float32).astype(
        jnp.bfloat16
    )
    rest_rows = jnp.dot(pick_bf, rest_all, preferred_element_type=jnp.float32).astype(jnp.bfloat16)
    block_rows = math.gcd(row_count, 16)
    block_count = row_count // block_rows

    def one_block(index):
        start = index * block_rows
        return param_block(
            lax.dynamic_slice_in_dim(params, start, block_rows, 0),
            lax.dynamic_slice_in_dim(grads, start, block_rows, 0),
            lax.dynamic_slice_in_dim(moments, start, block_rows, 1),
            lax.dynamic_slice_in_dim(row_new, start, block_rows, 0),
            lax.dynamic_slice_in_dim(col_rows, start, block_rows, 0),
            lax.dynamic_slice_in_dim(first_rows, start, block_rows, 0),
            lax.dynamic_slice_in_dim(rest_rows, start, block_rows, 0),
            lax.dynamic_slice_in_dim(scale_rows, start, block_rows, 0),
        )

    update = lax.map(one_block, lax.iota(jnp.int32, block_count)).reshape(params.shape)
    return (update, row_new, col_new, hidden_new, cell_new)


def solution(mesh):
    placed = (
        P(("fsdp", "rep"), None),
        P(("fsdp", "rep"), None),
        P(None, ("fsdp", "rep"), None),
        P(("fsdp", "rep")),
        P(),
        P(),
        P("fsdp", None),
        P("fsdp", None),
        P("fsdp", None),
        P(),
        P(),
        P(),
        P(),
        P(),
    )
    return jax.shard_map(
        on_device,
        mesh=mesh,
        in_specs=placed,
        out_specs=(
            P(("fsdp", "rep"), None),
            P(("fsdp", "rep")),
            P("fsdp", None),
            P("fsdp", None),
            P("fsdp", None),
        ),
        check_vma=False,
    )
```

profile of v0, /device:TPU:6, one launch (start us, length us, event | category | flops | bytes accessed | tf_op | source)
XLA Modules:
  0.0 246.5 jit_solution(8902016919694173329)
XLA Ops:
  7.2 1.3 multiply_reduce_fusion.1
  8.5 1.7 fusion.32
  12.1 3.2 %fusion.28 = f32[128,3584]{1,0:T(8,128)} fusion(bf16[48,3584]{1,0:T(8,128)(2,1)} %param.17, s32[128]{0:T(128)S(1)} %copy-done.8, s32[48]{0:T(128)S(1)} %convert_reduce_fusion), kind=kOutput, calls=%fused_computation.61 | convolution fusion | flops 264591360 | bytes 2179776 | tf_op jit(solution)/shard_map/ri,rc->ic/dot_general | solution.py:203
  15.6 2.9 %pad_maximum_fusion = f32[128,3592]{1,0:T(8,128)} fusion(f32[128,8]{1,0:T(8,128)S(1)} %fusion.44, f32[128,3584]{1,0:T(8,128)} %fusion.28), kind=kLoop, calls=%fused_computation.47 | loop fusion | flops 459776 | bytes 3678208 | tf_op jit(solution)/shard_map/concatenate | solution.py:29
  18.5 3.3 %reshape.222 = f32[64,2,3592]{2,1,0:T(2,128)} reshape(f32[128,3592]{1,0:T(8,128)} %pad_maximum_fusion) | data formatting | bytes 3678208 | tf_op jit(solution)/shard_map/reshape | solution.py:14
  21.8 16.8 %all-to-all-start = ((f32[64,2,3592]{2,1,0:T(2,128)}), f32[64,2,3592]{2,1,0:T(2,128)}, u32[]{:S(2)}, u32[]{:S(2)}) async-start(f32[64,2,3592]{2,1,0:T(2,128)} %reshape.222), calls=%async_computation | async-start | bytes 3801088 | tf_op jit(solution)/shard_map/all_to_all | solution.py:20
  38.7 48.2 %all-to-all-done = f32[64,2,3592]{2,1,0:T(2,128)} async-done(((f32[64,2,3592]{2,1,0:T(2,128)}), f32[64,2,3592]{2,1,0:T(2,128)}, u32[]{:S(2)}, u32[]{:S(2)}) %all-to-all-start) | async-done | bytes 1839136 | tf_op jit(solution)/shard_map/all_to_all | solution.py:20
  86.9 2.1 reduce_sum.139
  90.0 4.8 %all-to-all-start.1 = ((f32[8,1,7184]{2,1,0:T(1,128)}), f32[8,1,7184]{2,1,0:T(1,128)S(1)}, u32[]{:S(2)}, u32[]{:S(2)}) async-start(f32[8,1,7184]{2,1,0:T(1,128)} %broadcast_in_dim.18), calls=%async_computation.1 | async-start | bytes 466944 | tf_op jit(solution)/shard_map/all_to_all | solution.py:35
  95.0 4.9 %all-to-all-done.1 = f32[8,1,7184]{2,1,0:T(1,128)S(1)} async-done(((f32[8,1,7184]{2,1,0:T(1,128)}), f32[8,1,7184]{2,1,0:T(1,128)S(1)}, u32[]{:S(2)}, u32[]{:S(2)}) %all-to-all-start.1) | async-done | bytes 229920 | tf_op jit(solution)/shard_map/all_to_all | solution.py:35
  103.2 47.6 %all-gather = bf16[64,2,384]{2,1,0:T(2,128)(2,1)S(1)} all-gather(bf16[1,2,384]{2,1,0:T(2,128)(2,1)S(1)} %maximum_bitcast_fusion), channel_id=1, replica_groups=mesh['fsdp'=64,'rep'=8] {'fsdp'}, dimensions={0}, use_global_device_ids=true | all-gather | bytes 99840 | tf_op jit(solution)/shard_map/all_gather | solution.py:57
  151.2 29.5 %all-gather.4.cloned.1.call-done = f32[64,2,3588]{2,1,0:T(2,128)} async-done(((f32[1,2,3588]{2,1,0:T(2,128)}), f32[64,2,3588]{2,1,0:T(2,128)}) %all-gather.4.cloned.1.call-update) | async-done | bytes 1837072 | tf_op jit(solution)/shard_map/all_gather | solution.py:57
  180.7 3.5 %reshape.233 = f32[128,3588]{1,0:T(8,128)} reshape(f32[64,2,3588]{2,1,0:T(2,128)} %all-gather.4.cloned.1.call-done) | data formatting | bytes 3674112
  184.2 3.2 %fusion.25 = f32[48,3584]{1,0:T(8,128)} fusion(f32[128,3588]{1,0:T(8,128)} %reshape.233, s32[128]{0:T(128)S(1)} %copy-done.8, s32[48]{0:T(128)S(1)} %convert_reduce_fusion), kind=kOutput, calls=%fused_computation.48 | convolution fusion | flops 264247296 | bytes 2523840 | tf_op jit(solution)/shard_map/dot_general | solution.py:223
  188.4 50.7 %while.10 = (s32[]{:T(128)}, f32[3,16,3584]{2,1,0:T(8,128)}, s32[3]{0:T(128)S(1)}, bf16[48,128]{1,0:T(8,128)(2,1)S(1)}, bf16[48,256]{1,0:T(8,128)(2,1)S(1)}, /*i...) while((s32[]{:T(128)}, f32[3,16,3584]{2,1,0:T(8,128)}, ...), condition=%wide.region_16.17_spmd, body=%wide.region_15.16_spmd.sunk | while | flops 47481352 | bytes 11315383 | solution.py:246
  191.0 1.3 fusion.90
  195.3 5.5 %stack.79 = bf16[16,8,3584]{2,1,0:T(8,128)(2,1)} concatenate(bf16[16,1,3584]{2,1,0:T(2,128)(2,1)S(1)} %copy.188, bf16[16,1,3584]{2,1,0:T(2,128)(2,1)S(1)} %copy.189, bf16[16,1,3584]{2,1,0:T(2,128)(2,1)S(1)} %copy.190, bf16[16,1,3584]{2,1,0:T(2,128)(2,1)S(1)} %copy.191, bf16[16,1,3584]{2,1,0:T(2,128)(2,1)S(1)} %copy.192, bf16[16,1,3584]{2,1,0:T(2,128)(2,1)} %fusion.91, ...), dimensions={1} | concatenate | bytes 1835008 | tf_op jit(solution)/shard_map/while/body/eval_jaxpr/stack | solution.py:131
  201.3 2.8 %fusion.92 = f32[16,3,3584]{2,1,0:T(4,128)S(1)} fusion(bf16[16,32,3]{1,2,0:T(4,128)(2,1)S(1)} %copy.187, bf16[16,8,32]{2,1,0:T(8,128)(2,1)S(1)} %reshape.238, bf16[16,8,3584]{2,1,0:T(8,128)(2,1)} %stack.79, f32[16,32]{1,0:T(8,128)S(1)} %dynamic-slice_convert_fusion.5), kind=kOutput, calls=%fused_computation.1.clone.1 | convolution fusion | flops 45875200 | bytes 1618944 | tf_op jit(solution)/shard_map/while/body/eval_jaxpr/bhc,bho->boc/dot_general | solution.py:153
  207.9 1.3 fusion.90
  212.2 5.5 %stack.79 = bf16[16,8,3584]{2,1,0:T(8,128)(2,1)} concatenate(bf16[16,1,3584]{2,1,0:T(2,128)(2,1)S(1)} %copy.188, bf16[16,1,3584]{2,1,0:T(2,128)(2,1)S(1)} %copy.189, bf16[16,1,3584]{2,1,0:T(2,128)(2,1)S(1)} %copy.190, bf16[16,1,3584]{2,1,0:T(2,128)(2,1)S(1)} %copy.191, bf16[16,1,3584]{2,1,0:T(2,128)(2,1)S(1)} %copy.192, bf16[16,1,3584]{2,1,0:T(2,128)(2,1)} %fusion.91, ...), dimensions={1} | concatenate | bytes 1835008 | tf_op jit(solution)/shard_map/while/body/eval_jaxpr/stack | solution.py:131
  218.2 2.8 %fusion.92 = f32[16,3,3584]{2,1,0:T(4,128)S(1)} fusion(bf16[16,32,3]{1,2,0:T(4,128)(2,1)S(1)} %copy.187, bf16[16,8,32]{2,1,0:T(8,128)(2,1)S(1)} %reshape.238, bf16[16,8,3584]{2,1,0:T(8,128)(2,1)} %stack.79, f32[16,32]{1,0:T(8,128)S(1)} %dynamic-slice_convert_fusion.5), kind=kOutput, calls=%fused_computation.1.clone.1 | convolution fusion | flops 45875200 | bytes 1618944 | tf_op jit(solution)/shard_map/while/body/eval_jaxpr/bhc,bho->boc/dot_general | solution.py:153
  224.8 1.3 fusion.90
  229.1 5.5 %stack.79 = bf16[16,8,3584]{2,1,0:T(8,128)(2,1)} concatenate(bf16[16,1,3584]{2,1,0:T(2,128)(2,1)S(1)} %copy.188, bf16[16,1,3584]{2,1,0:T(2,128)(2,1)S(1)} %copy.189, bf16[16,1,3584]{2,1,0:T(2,128)(2,1)S(1)} %copy.190, bf16[16,1,3584]{2,1,0:T(2,128)(2,1)S(1)} %copy.191, bf16[16,1,3584]{2,1,0:T(2,128)(2,1)S(1)} %copy.192, bf16[16,1,3584]{2,1,0:T(2,128)(2,1)} %fusion.91, ...), dimensions={1} | concatenate | bytes 1835008 | tf_op jit(solution)/shard_map/while/body/eval_jaxpr/stack | solution.py:131
  235.1 2.8 %fusion.92 = f32[16,3,3584]{2,1,0:T(4,128)S(1)} fusion(bf16[16,32,3]{1,2,0:T(4,128)(2,1)S(1)} %copy.187, bf16[16,8,32]{2,1,0:T(8,128)(2,1)S(1)} %reshape.238, bf16[16,8,3584]{2,1,0:T(8,128)(2,1)} %stack.79, f32[16,32]{1,0:T(8,128)S(1)} %dynamic-slice_convert_fusion.5), kind=kOutput, calls=%fused_computation.1.clone.1 | convolution fusion | flops 45875200 | bytes 1618944 | tf_op jit(solution)/shard_map/while/body/eval_jaxpr/bhc,bho->boc/dot_general | solution.py:153
  (145 shorter events, 28.1 us)
Async XLA Ops:
  7.2 94.7 %copy-start = (bf16[512,2048]{1,0:T(8,128)(2,1)S(1)}, bf16[512,2048]{1,0:T(8,128)(2,1)}, u32[]{:S(2)}) copy-start(bf16[512,2048]{1,0:T(8,128)(2,1)} %param.26) | copy-start | bytes 6291460
  7.2 4.3 %copy-start.11 = (s32[128]{0:T(128)S(1)}, s32[128]{0:T(128)}, u32[]{:S(2)}) copy-start(s32[128]{0:T(128)} %param.20) | copy-start | bytes 1540
  7.2 4.9 %copy-start.8 = (s32[128]{0:T(128)S(1)}, s32[128]{0:T(128)}, u32[]{:S(2)}) copy-start(s32[128]{0:T(128)} %param.21) | copy-start | bytes 1540
  21.8 65.1 %all-to-all-start = ((f32[64,2,3592]{2,1,0:T(2,128)}), f32[64,2,3592]{2,1,0:T(2,128)}, u32[]{:S(2)}, u32[]{:S(2)}) async-start(f32[64,2,3592]{2,1,0:T(2,128)} %reshape.222), calls=%async_computation | async-start | bytes 3801088 | tf_op jit(solution)/shard_map/all_to_all | solution.py:20
  38.7 61.7 %copy-start.6 = (f32[2,3584]{1,0:T(2,128)S(1)}, f32[2,3584]{1,0:T(2,128)}, u32[]{:S(2)}) copy-start(f32[2,3584]{1,0:T(2,128)} %param.22) | copy-start | bytes 86020
  38.7 62.8 %copy-start.12 = (f32[48]{0:T(128)S(1)}, f32[48]{0:T(128)}, u32[]{:S(2)}) copy-start(f32[48]{0:T(128)} %param.19) | copy-start | bytes 580
  38.7 63.0 %copy-start.4 = (bf16[10,2048]{1,0:T(8,128)(2,1)S(1)}, bf16[10,2048]{1,0:T(8,128)(2,1)}, u32[]{:S(2)}) copy-start(bf16[10,2048]{1,0:T(8,128)(2,1)} %param.25) | copy-start | bytes 122884
  38.7 63.1 %copy-start.7 = (f32[2048]{0:T(1024)S(1)}, f32[2048]{0:T(1024)}, u32[]{:S(2)}) copy-start(f32[2048]{0:T(1024)} %param.27) | copy-start | bytes 24580
  38.7 63.1 %copy-start.9 = (f32[2,512]{1,0:T(2,128)S(1)}, f32[2,512]{1,0:T(2,128)}, u32[]{:S(2)}) copy-start(f32[2,512]{1,0:T(2,128)} %param.23) | copy-start | bytes 12292
  89.0 13.2 %copy-start.10 = (f32[2,512]{1,0:T(2,128)S(1)}, f32[2,512]{1,0:T(2,128)}, u32[]{:S(2)}) copy-start(f32[2,512]{1,0:T(2,128)} %param.24) | copy-start | bytes 12292
  89.0 13.9 %copy-start.2 = (bf16[512,128]{1,0:T(8,128)(2,1)S(1)}, bf16[512,128]{1,0:T(8,128)(2,1)}, u32[]{:S(2)}) copy-start(bf16[512,128]{1,0:T(8,128)(2,1)} %param.29) | copy-start | bytes 393220
  89.2 13.8 %copy-start.1 = (bf16[512,256]{1,0:T(8,128)(2,1)S(1)}, bf16[512,256]{1,0:T(8,128)(2,1)}, u32[]{:S(2)}) copy-start(bf16[512,256]{1,0:T(8,128)(2,1)} %param.28) | copy-start | bytes 786436
  90.0 9.9 %all-to-all-start.1 = ((f32[8,1,7184]{2,1,0:T(1,128)}), f32[8,1,7184]{2,1,0:T(1,128)S(1)}, u32[]{:S(2)}, u32[]{:S(2)}) async-start(f32[8,1,7184]{2,1,0:T(1,128)} %broadcast_in_dim.18), calls=%async_computation.1 | async-start | bytes 466944 | tf_op jit(solution)/shard_map/all_to_all | solution.py:35
  94.7 86.0 %all-gather.4.cloned.1.call-start = ((), (), s32[]{:S(2)}) async-start(), calls=%async_computation.2 | async-start | bytes 1930240 | tf_op jit(solution)/shard_map/all_gather | solution.py:57
  100.6 83.6 %copy-start.3 = (f32[2,3584]{1,0:T(2,128)}, f32[2,3584]{1,0:T(2,128)S(1)}, u32[]{:S(2)}) copy-start(f32[2,3584]{1,0:T(2,128)S(1)} %get-tuple-element.150) | copy-start | bytes 86020
  102.9 81.4 %copy-start.5 = (f32[2,512]{1,0:T(2,128)}, f32[2,512]{1,0:T(2,128)S(1)}, u32[]{:S(2)}) copy-start(f32[2,512]{1,0:T(2,128)S(1)} %get-tuple-element.148) | copy-start | bytes 12292
  239.2 0.5 copy-start.13
Sparse Core Ops, SparseCore 0:
  101.5 79.1 all-gather.3
where the time goes:
time: 249 us; the launch traced here: 247 us
  waiting for transfers between devices  82.6 us (33%)
  blocking collectives  47.6 us (19%)
  local copies, waits for them, and re-layouts  37 us (15%)
  other arithmetic  23.7 us (10%)
  starting transfers between devices  21.6 us (9%)
  matrix products  17.3 us (7%)
  between operations  14.3 us (6%)
    all_to_all x1, waiting for transfers between devices, sent_and_summed(): lax.all_to_all(parts, axis, split_axis=0, concat_axis=0, tiled=True)  48.2 us
    all_gather x1, blocking collectives, in_one_piece(): lax.all_gather(both, axis, axis=dim, tiled=True)  47.6 us
    all_gather x1, waiting for transfers between devices, in_one_piece(): lax.all_gather(both, axis, axis=dim, tiled=True)  29.5 us
    another operation x24, local copies, waits for them, and re-layouts, param_block(): jnp.stack([grad_norm, mom_norm, mom_f[1] * inv_rms, mom_f[2] * inv_rms, g...  22.3 us
    all_to_all x1, starting transfers between devices, sent_and_summed(): lax.all_to_all(parts, axis, split_axis=0, concat_axis=0, tiled=True)  16.8 us
    dot_general x3, matrix products, param_block(): jnp.einsum('bhc,bho->boc', hidden_units, w_second, preferred_element_type...  8.41 us
  transfers between devices with their start and end apart: 3, of which 3 were waited for; matrix products, arithmetic and copies ran while one was open for 1% of the time, Pallas kernels for 0%

commit v1 on v0

v1 whole, which is shorter than its diff:
```python
import functools
import math

import jax
import jax.numpy as jnp
from jax import lax
from jax.experimental import pallas as pl
from jax.experimental.pallas import tpu as pltpu
from jax.sharding import PartitionSpec as P

EPS = 1e-06
DECAY = 0.9
FIN = 8
F32 = jnp.float32
BF16 = jnp.bfloat16
MESH = pl.DeviceIdType.MESH
VMEM = pltpu.VMEM
LIMIT = 60 * 1024 * 1024


class Sizes:
    def __init__(self, mesh, params, col_acc, hidden_state, rest):
        self.fsdp, self.rep = mesh.shape["fsdp"], mesh.shape["rep"]
        self.nz = self.ny = math.isqrt(self.fsdp)
        self.nt = col_acc.shape[0]
        self.own = self.nt // self.fsdp
        self.rows = params.shape[0] // (self.fsdp * self.rep)
        self.c = params.shape[1]
        self.hid = hidden_state.shape[1]
        self.hm = rest.shape[1] // 4
        self.sl = self.c // (self.rep - 1)
        self.cw = self.c + 128
        self.w = (self.c + 3 * self.hid) // 2
        self.all_rows = self.rows + 8
        assert self.own == 2 and self.sl % 128 == 0 and self.w % 128 == 0 and self.rows % 16 == 0


def iota(shape, dim):
    return lax.broadcasted_iota(jnp.int32, shape, dim)


def fiota(shape, dim):
    return iota(shape, dim).astype(F32)


def rem(a, b):
    return lax.rem(a, jnp.int32(b))


def div(a, b):
    return lax.div(a, jnp.int32(b))


def slot_bounds(s, lens, order):
    a, b = iota((s.nt, s.nt), 0), iota((s.nt, s.nt), 1)
    lens_col = jnp.sum(jnp.where(a == b, lens, 0.0), axis=1, keepdims=True)
    ids = a.astype(F32)
    end = jnp.sum(jnp.where(ids <= order, lens_col, 0.0), axis=0, keepdims=True)
    size = jnp.sum(jnp.where(ids == order, lens_col, 0.0), axis=0, keepdims=True)
    return end - size, end


def slot_hits(pos, start, end):
    return jnp.where((pos >= start) & (pos < end), 1.0, 0.0)


def ranges(pos, start, end):
    hits = slot_hits(pos, start, end)
    first = jnp.sum(hits * start, axis=1, keepdims=True)
    last = jnp.sum(hits * end, axis=1, keepdims=True)
    return first, last, hits


def split2(x):
    hi = x.astype(BF16)
    return hi, (x - hi.astype(F32)).astype(BF16)


def restack(t):
    lane = iota(t.shape, 1)
    both = t + pltpu.roll(t, 120, 1)
    hi = both.astype(BF16).astype(F32)
    low = pltpu.roll(both - hi, 8, 1)
    return jnp.where(lane < 8, hi, jnp.where(lane < 16, low, 0.0))


def local_kernel(s, params, grads, moments, row_acc, lens, order, col_acc, hidden, cell,
                 row_new, row_var, gs, ht, ag):
    device = lax.axis_index("fsdp") * s.rep + lax.axis_index("rep")
    start, end = slot_bounds(s, lens[...], order[...])
    own = jnp.concatenate([v.astype(BF16) for v in (col_acc[...], hidden[...])] + list(split2(cell[...])), axis=1)
    ag[0] = own[:, : s.w]
    ag[1] = own[:, s.w :]
    sums = [jnp.zeros((s.rows, 1), F32) for _ in range(8)]
    for j in range(s.rep - 1):
        cols = pl.ds(j * s.sl, s.sl)
        g, p = grads[:, cols].astype(F32), params[:, cols]
        m = [moments[k, :, cols].astype(F32) for k in range(3)]
        sq = g * g
        gs[j] = sq.astype(BF16)
        for k, v in enumerate((sq, m[0] * m[0], m[1] * m[1], m[2] * m[2], p * p, g * m[0], g * m[2], m[0] * m[2])):
            sums[k] = sums[k] + jnp.sum(v, axis=1, keepdims=True)
    lane = iota((s.rows, 128), 1)
    stats = jnp.zeros((s.rows, 128), F32)
    for k in range(8):
        hi, low = split2(sums[k])
        stats = jnp.where(lane == k, hi.astype(F32), stats)
        stats = jnp.where(lane == k + 8, low.astype(F32), stats)
    gs[s.rep - 1] = jnp.zeros((s.rows, s.sl), BF16)
    gs[s.rep - 1, :, :128] = stats.astype(BF16)
    a, b = iota((s.rows, s.rows), 0), iota((s.rows, s.rows), 1)
    acc_col = jnp.sum(jnp.where(a == b, row_acc[...], 0.0), axis=1, keepdims=True)
    new_col = DECAY * acc_col + (1.0 - DECAY) * (sums[0] / s.c)
    row_new[...] = jnp.sum(jnp.where(a == b, new_col, 0.0), axis=0, keepdims=True)
    row_var[...] = jnp.broadcast_to(new_col, (s.rows, 128))
    base = (device * s.rows).astype(F32)
    which = fiota((16, 1), 0)
    pos = jnp.where(which == 0.0, base, jnp.where(which == 1.0, base + (s.rows - 1), -1.0))
    first, last, _ = ranges(pos, start, end)
    here = base + fiota((1, s.rows), 1)
    pick = slot_hits(here, first, last).astype(BF16)
    for j in range(s.rep - 1):
        part = jnp.dot(pick, gs[j], preferred_element_type=F32)
        ht[:, j * s.sl : (j + 1) * s.sl] = part[:2].astype(BF16)
    part = jnp.dot(pick, gs[s.rep - 1, :, :128], preferred_element_type=F32)
    ht[:, s.c :] = restack(part)[:2].astype(BF16)


def remote(src, dst, sems, k, fsdp, rep):
    return pltpu.make_async_remote_copy(
        src_ref=src, dst_ref=dst, send_sem=sems.at[0, k], recv_sem=sems.at[1, k],
        device_id={"fsdp": fsdp, "rep": rep}, device_id_type=MESH,
    )


def comm_kernel(s, lens, order, ht, gs, ag, htall, nb, table, xbuf,
                piece, nbsrc, gx, zsrc, zbuf, ysrc, ybuf, xsrc,
                s_ht, s_nb, s_p, s_t, s_d, s_g, s_z, s_y, s_x):
    f, r = lax.axis_index("fsdp"), lax.axis_index("rep")
    z, y, core = div(f, s.ny), rem(f, s.ny), rem(r, 2)
    partner = r + 1 - 2 * core
    nxt, prv = rem(f + 1, s.fsdp), rem(f + s.fsdp - 1, s.fsdp)

    def at_rep(k):
        return rem(r + k, s.rep)

    def at_y(k):
        return z * s.ny + rem(y + k, s.ny)

    def at_z(k):
        return rem(z + k, s.nz) * s.ny + y

    def first_axis(k):
        return (1 - core) * at_y(k) + core * at_z(k)

    def second_axis(k):
        return (1 - core) * at_z(k) + core * at_y(k)

    barrier = pltpu.get_barrier_semaphore()
    peers = [(f, at_rep(k)) for k in range(1, s.rep)]
    peers += [(at_y(k), r) for k in range(1, s.ny)] + [(at_z(k), r) for k in range(1, s.nz)]
    peers += [(nxt, r), (prv, r)]
    for pf, pr in peers:
        pl.semaphore_signal(barrier, inc=1, device_id={"fsdp": pf, "rep": pr}, device_id_type=MESH)
    pl.semaphore_wait(barrier, len(peers))

    reps, ys, zs = range(1, s.rep), range(1, s.ny), range(1, s.nz)
    c_p = [remote(ag.at[core], piece.at[k], s_p, k, first_axis(k), r) for k in ys]
    c_ht = [remote(ht, htall.at[k], s_ht, k, f, at_rep(k)) for k in reps]
    c_g = [remote(gs.at[at_rep(k)], gx.at[k], s_g, k, f, at_rep(k)) for k in reps]
    for c in c_p + c_ht + c_g:
        c.start()
    htall[0] = ht[...]
    piece[0] = ag[core]
    gx[0] = gs[r]

    start, end = slot_bounds(s, lens[...], order[...])
    group = s.rep * s.rows
    base = (f * group).astype(F32)
    which = fiota((8, 1), 0)
    first, last, _ = ranges(jnp.where(which == 0.0, base + (group - 1), base), start, end)
    coef = []
    for k in range(s.rep):
        at = base + (rem(r + s.rep - k, s.rep) * s.rows).astype(F32)
        head = jnp.where((at >= first) & (at < last), 1.0, 0.0)
        tail = jnp.where((at + (s.rows - 1) >= first) & (at + (s.rows - 1) < last), 1.0, 0.0)
        coef.append((head, tail * (1.0 - head)))
    for c in c_ht:
        c.wait_recv()
    acc = jnp.zeros((2, s.cw), F32)
    for k in range(s.rep):
        both = htall[k].astype(F32)
        acc = acc + coef[k][0][:2] * both[0:1] + coef[k][1][:2] * both[1:2]
    acc = jnp.concatenate([acc[:, : s.c], restack(acc[:, s.c :])], axis=1)
    nbsrc[0] = jnp.broadcast_to(acc[0:1], (2, s.cw)).astype(BF16)
    nbsrc[1] = jnp.broadcast_to(acc[1:2], (2, s.cw)).astype(BF16)
    c_nb = [remote(nbsrc.at[0], nb.at[0], s_nb, 0, nxt, r), remote(nbsrc.at[1], nb.at[1], s_nb, 1, prv, r)]
    for c in c_nb:
        c.start()

    for c in c_p:
        c.wait_recv()
    table[core, 0] = jnp.concatenate([piece[k] for k in range(s.ny)], axis=0)
    c_t = [remote(table.at[core, 0], table.at[core, k], s_t, k, second_axis(k), r) for k in zs]
    c_d = [remote(table.at[core, k], table.at[core, k], s_d, k, f, partner) for k in range(s.nz)]
    for c in c_t + c_d[:1]:
        c.start()

    for c in c_g:
        c.wait_recv()
    per = 2 * s.ny
    a, b = iota((s.nt, s.nt), 0), iota((s.nt, s.nt), 1)
    slot = rem(rem(z + div(a, per), s.nz) * per + rem(a, per), s.nt)
    order_col = jnp.sum(jnp.where(b == slot, order[...], 0.0), axis=1, keepdims=True)
    ids = b.astype(F32)
    end_col = jnp.sum(jnp.where(ids <= order_col, lens[...], 0.0), axis=1, keepdims=True)
    start_col = end_col - jnp.sum(jnp.where(ids == order_col, lens[...], 0.0), axis=1, keepdims=True)
    sums = jnp.zeros((s.nt, s.sl), F32)
    for k in range(s.rep):
        at = base + (rem(r + s.rep - k, s.rep) * s.rows).astype(F32) + fiota((1, s.rows), 1)
        sums = sums + jnp.dot(slot_hits(at, start_col, end_col).astype(BF16), gx[k], preferred_element_type=F32)
    for k in range(s.nz):
        zsrc[k] = sums[k * per : (k + 1) * per].astype(BF16)
    c_z = [remote(zsrc.at[k], zbuf.at[k], s_z, k, at_z(k), r) for k in zs]
    for c in c_z:
        c.start()
    zbuf[0] = zsrc[0]

    for k in zs:
        c_t[k - 1].wait_recv()
        c_d[k].start()

    for c in c_z:
        c.wait_recv()
    total = zbuf[0].astype(F32)
    for k in zs:
        total = total + zbuf[k].astype(F32)
    ysrc[...] = total.astype(BF16)
    c_y = [remote(ysrc, ybuf.at[k], s_y, k, at_y(k), r) for k in ys]
    for c in c_y:
        c.start()
    for c in c_y:
        c.wait_recv()
    total = ysrc[...].astype(F32)
    for k in ys:
        total = total + ybuf[k].astype(F32)
    row = iota((per, s.sl), 0)
    mine = [jnp.sum(jnp.where(row == 2 * y + j, total, 0.0), axis=0, keepdims=True) for j in range(2)]
    row = iota((8, s.sl), 0)
    out = jnp.where(row == 0, mine[0], jnp.where(row == 1, mine[1], 0.0))
    xsrc[...] = out
    c_x = [remote(xsrc, xbuf.at[r], s_x, k, f, at_rep(k)) for k in reps]
    for c in c_x:
        c.start()
    xbuf[r] = out

    for c in c_x + c_d + c_nb:
        c.wait_recv()
    for c in c_p + c_ht + c_g + c_nb + c_t + c_d + c_z + c_y + c_x:
        c.wait_send()


def final_kernel(s, params, grads, moments, row_var, lens, order, col_acc, hidden, cell, w_in, w_rec, bias, w_first,
                 w_rest, gs, htall, nb, table, xbuf,
                 update, col_new, hidden_new, cell_new,
                 cols, ht16, gen, pick_w2):
    f, r = lax.axis_index("fsdp"), lax.axis_index("rep")
    z, y = div(f, s.ny), rem(f, s.ny)
    rows, n, nt, chunks = s.rows, s.all_rows, s.nt, s.rep - 1
    start, end = slot_bounds(s, lens[...], order[...])
    base = ((f * s.rep + r) * rows).astype(F32)
    row = iota((n, 1), 0)
    pos = jnp.where(row < rows, base + row.astype(F32), -1.0)
    lane = iota((n, nt), 1)
    mine = jnp.where((row >= rows) & (row < rows + 2) & (lane == row - rows + 2 * f), 1.0, 0.0)
    hits = slot_hits(pos, start, end) + mine
    first = jnp.sum(hits * start, axis=1, keepdims=True)
    last = jnp.sum(hits * end, axis=1, keepdims=True)
    length = jnp.maximum(last - first, 1.0)
    slot_of = jnp.sum(hits * lane.astype(F32), axis=1, keepdims=True)
    last = jnp.where(row < rows, last, first)

    group = (f * (s.rep * rows)).astype(F32)
    same = slot_hits(base + fiota((1, rows), 1), first, last).astype(BF16)
    la = iota((1, 2 * s.rep), 1)
    src = rem(r + s.rep - div(la, 2), s.rep)
    head = group + (src * rows).astype(F32)
    in_head = slot_hits(head, first, last)
    in_tail = slot_hits(head + (rows - 1), first, last) * (1.0 - in_head)
    shared = jnp.where(div(la, 2) == 0, 0.0, jnp.where(rem(la, 2) == 0, in_head, in_tail)).astype(BF16)
    before = slot_hits(group - 1.0, first, last)
    after = slot_hits(group + s.rep * rows, first, last)

    for k in range(s.rep):
        ht16[2 * k : 2 * k + 2, :] = htall[k].astype(F32)

    per = 2 * s.ny
    zz, yy, jj = div(lane, per), rem(div(lane, 2), s.ny), rem(lane, 2)
    slot_a = rem(z + s.nz - zz, s.nz) * per + rem(y + s.ny - yy, s.ny) * 2 + jj
    slot_b = rem(z + s.nz - yy, s.nz) * per + rem(y + s.ny - zz, s.ny) * 2 + jj
    hit_a = jnp.where(slot_a.astype(F32) == slot_of, 1.0, 0.0).astype(BF16)
    hit_b = jnp.where(slot_b.astype(F32) == slot_of, 1.0, 0.0).astype(BF16)
    top = iota((8, 1), 0)

    def own_rows(a):
        return jnp.where(top == 0, a[0:1], jnp.where(top == 1, a[1:2], 0.0))

    def held(lo, hi, own):
        parts = []
        for half, hit in ((0, hit_a), (1, hit_b)):
            a, b = max(lo, half * s.w) - half * s.w, min(hi, (half + 1) * s.w) - half * s.w
            if a < b:
                t = table[half, :, :, a:b].reshape(nt, b - a)
                parts.append(jnp.dot(hit[:rows], t, preferred_element_type=F32))
        got = parts[0] if len(parts) == 1 else jnp.concatenate(parts, axis=1)
        return jnp.concatenate([got, own_rows(own)], axis=0)

    def sums(g, lo, hi, total):
        out = jnp.dot(same[:rows], g, preferred_element_type=F32)
        out = out + jnp.dot(shared[:rows], ht16[: 2 * s.rep, lo:hi].astype(BF16), preferred_element_type=F32)
        out = out + before[:rows] * nb[0, :, lo:hi].astype(F32)[0:1] + after[:rows] * nb[1, :, lo:hi].astype(F32)[0:1]
        return jnp.concatenate([out, total], axis=0)

    total_col = jnp.zeros((n, 1), F32)
    total_sq = jnp.zeros((n, 1), F32)
    for j in range(chunks):
        lo, hi = j * s.sl, (j + 1) * s.sl
        got = sums(gs[j], lo, hi, xbuf[j])
        new = DECAY * held(lo, hi, col_acc[:, lo:hi]) + (1.0 - DECAY) * got / length
        cols[:, lo:hi] = new
        col_new[:, lo:hi] = new[rows : rows + 2]
        total_col = total_col + jnp.sum(new, axis=1, keepdims=True)
        total_sq = total_sq + jnp.sum(new * new, axis=1, keepdims=True)
    stats = sums(gs[chunks, :, :128], s.c, s.cw, xbuf[chunks, :, :128])
    means = [(stats[:, k : k + 1] + stats[:, k + 8 : k + 9]) / (length * s.c) for k in range(8)]
    col_mean = total_col / s.c
    col_square = total_sq / s.c
    feats = [jnp.log(means[k] + EPS) for k in range(5)]
    feats += [means[5] / jnp.sqrt(means[0] * means[1] + EPS), means[6] / jnp.sqrt(means[0] * means[3] + EPS),
              means[7] / jnp.sqrt(means[1] * means[3] + EPS), jnp.log(col_mean + EPS),
              jnp.log(col_square / (col_mean * col_mean))]
    feats = [v.astype(BF16).astype(F32) for v in feats]
    hid = held(s.c, s.c + s.hid, hidden[...]).astype(BF16)
    old = held(s.c + s.hid, s.c + 2 * s.hid, cell[...]) + held(s.c + 2 * s.hid, s.c + 3 * s.hid, jnp.zeros_like(cell[...]))

    def gate(k):
        lo, hi = k * s.hid, (k + 1) * s.hid
        out = jnp.dot(hid, w_rec[:, lo:hi], preferred_element_type=F32) + bias[:, lo:hi]
        w = w_in[:, lo:hi].astype(F32)
        for i, v in enumerate(feats):
            out = out + v * w[i : i + 1]
        return out

    now = jax.nn.sigmoid(gate(1)) * old + jax.nn.sigmoid(gate(0)) * jnp.tanh(gate(2))
    state = jax.nn.sigmoid(gate(3)) * jnp.tanh(now)
    hidden_new[...] = state[rows : rows + 2]
    cell_new[...] = now[rows : rows + 2]
    bf = state.astype(BF16)
    width = (FIN + 1 + 3) * s.hm
    gen[:, : FIN * s.hm] = jnp.dot(bf, w_first[...], preferred_element_type=F32)
    gen[:, FIN * s.hm :] = jnp.dot(bf, w_rest[...], preferred_element_type=F32)
    inv = [1.0 / jnp.sqrt(means[k][:rows] + EPS) for k in (0, 1, 4)]
    var = row_var[:, 0:1] / col_mean[:rows]

    m, deep = 8 * s.hm, 8 * (FIN + 2)
    lw = iota((m, width), 1)
    spread = jnp.where(rem(iota((m, 8), 0), 8) == iota((m, 8), 1), 1.0, 0.0).astype(BF16)
    keep = (rem(lw, s.hm) == div(iota((m, width), 0), 8)) & (lw < (FIN + 1) * s.hm)
    fold = jnp.where(div(iota((width, deep), 0), s.hm) == div(iota((width, deep), 1), 8), 1.0, 0.0).astype(BF16)
    diag1 = (rem(iota((m, deep), 0), 8) == rem(iota((m, deep), 1), 8)) & (iota((m, deep), 1) < 8 * (FIN + 1))
    diag2 = iota((8, m), 0) == rem(iota((8, m), 1), 8)
    for o in range(3):
        want = (FIN + 1) * s.hm + 3 * div(iota((width, m), 1), 8) + o
        pick_w2[o] = jnp.where(iota((width, m), 0) == want, 1.0, 0.0).astype(BF16)
    cols_scale = jnp.concatenate([var, inv[0], inv[1], inv[2]], axis=1)
    ht16[0:rows, 0:4] = cols_scale

    ones, zeros = jnp.ones((8, s.sl), F32), jnp.zeros((8, s.sl), F32)

    def block(i, carry):
        at = pl.multiple_of(i * 16, 16)
        made = gen[pl.ds(at, 16), :].astype(BF16).astype(F32)
        sc = ht16[pl.ds(at, 16), 0:128]
        weights = []
        for half in range(2):
            own = made[8 * half : 8 * half + 8].astype(BF16)
            y1 = jnp.where(keep, jnp.dot(spread, own, preferred_element_type=F32), 0.0).astype(BF16)
            w1 = jnp.where(diag1, jnp.dot(y1, fold, preferred_element_type=F32), 0.0).astype(BF16)
            w2 = [jnp.where(diag2, jnp.dot(own, pick_w2[o], preferred_element_type=F32), 0.0) for o in range(3)]
            weights.append((w1, jnp.concatenate(w2, axis=0).astype(BF16)))
        for j in range(chunks):
            lo, hi = j * s.sl, (j + 1) * s.sl
            g16 = grads[pl.ds(at, 16), lo:hi].astype(F32)
            m16 = [moments[k, pl.ds(at, 16), lo:hi].astype(F32) for k in range(3)]
            p16 = params[pl.ds(at, 16), lo:hi]
            c16 = cols[pl.ds(at, 16), lo:hi]
            for half in range(2):
                q = slice(8 * half, 8 * half + 8)
                g, m0, m1, m2, p, cn = g16[q], m16[0][q], m16[1][q], m16[2][q], p16[q], c16[q]
                rms = lax.rsqrt(cn * sc[q, 0:1] + EPS)
                gn, mn = g * rms, m0 * rms
                x = jnp.concatenate(
                    [gn, mn, m1 * rms, m2 * rms, g * sc[q, 1:2], m0 * sc[q, 2:3], p * sc[q, 3:4], gn * mn, ones, zeros],
                    axis=0,
                ).astype(BF16)
                w1, w2 = weights[half]
                unit = jnp.maximum(jnp.dot(w1, x, preferred_element_type=F32), 0.0).astype(BF16)
                o = jnp.dot(w2, unit, preferred_element_type=F32)
                out = o[0:8] * jnp.exp(jnp.tanh(o[8:16])) * jax.nn.sigmoid(o[16:24])
                update[pl.ds(pl.multiple_of(at + 8 * half, 8), 8), lo:hi] = out
        return carry

    lax.fori_loop(0, rows // 16, block, 0)


def on_device(s, params, grads, moments, row_acc, lengths, tensor_order, col_acc, hidden_state, cell_state,
              lstm_in, lstm_rec, lstm_bias, hyper_first, hyper_rest):
    shape = jax.ShapeDtypeStruct
    rows = s.rows
    lens = lengths.astype(F32).reshape(1, s.nt)
    order = tensor_order.astype(F32).reshape(1, s.nt)
    limit = pltpu.CompilerParams(vmem_limit_bytes=LIMIT)
    row_new, row_var, gs, ht, ag = pl.pallas_call(
        functools.partial(local_kernel, s),
        out_shape=(
            shape((1, rows), F32), shape((rows, 128), F32), shape((s.rep, rows, s.sl), BF16), shape((2, s.cw), BF16),
            shape((2, 2, s.w), BF16),
        ),
        compiler_params=limit,
        name="local",
    )(params, grads, moments, row_acc.reshape(1, rows), lens, order, col_acc, hidden_state, cell_state)

    def sems(k):
        return pltpu.SemaphoreType.DMA((2, k))

    per = 2 * s.ny
    htall, nb, table, xbuf = pl.pallas_call(
        functools.partial(comm_kernel, s),
        out_shape=(
            shape((s.rep, 2, s.cw), BF16), shape((2, 2, s.cw), BF16), shape((2, s.nz, per, s.w), BF16),
            shape((s.rep, 8, s.sl), F32),
        ),
        in_specs=[pl.BlockSpec(memory_space=VMEM)] * 5,
        out_specs=(pl.BlockSpec(memory_space=VMEM),) * 4,
        scratch_shapes=[
            VMEM((s.ny, 2, s.w), BF16), VMEM((2, 2, s.cw), BF16), VMEM((s.rep, rows, s.sl), BF16),
            VMEM((s.nz, per, s.sl), BF16), VMEM((s.nz, per, s.sl), BF16), VMEM((per, s.sl), BF16),
            VMEM((s.ny, per, s.sl), BF16), VMEM((8, s.sl), F32),
            sems(s.rep), sems(2), sems(s.ny), sems(s.nz), sems(s.nz), sems(s.rep), sems(s.nz), sems(s.ny), sems(s.rep),
        ],
        compiler_params=pltpu.CompilerParams(collective_id=0, has_side_effects=True, vmem_limit_bytes=LIMIT),
        name="exchange",
    )(lens, order, ht, gs, ag)
    width = (FIN + 4) * s.hm
    update, col_new, hidden_new, cell_new = pl.pallas_call(
        functools.partial(final_kernel, s),
        out_shape=(
            shape(params.shape, F32), shape(col_acc.shape, F32), shape(hidden_state.shape, F32),
            shape(cell_state.shape, F32),
        ),
        scratch_shapes=[
            VMEM((s.all_rows, s.c), F32), VMEM((max(2 * s.rep, rows), s.cw), F32), VMEM((s.all_rows, width), F32),
            VMEM((3, width, 8 * s.hm), BF16),
        ],
        compiler_params=limit,
        name="networks",
    )(params, grads, moments, row_var, lens, order, col_acc, hidden_state, cell_state, lstm_in, lstm_rec,
      lstm_bias.reshape(1, -1), hyper_first, hyper_rest, gs, htall, nb, table, xbuf)
    return update, row_new.reshape(rows), col_new, hidden_new, cell_new


def solution(mesh):
    rowwise, owned, everywhere = P(("fsdp", "rep"), None), P("fsdp", None), P()

    def step(params, grads, moments, row_acc, lengths, tensor_order, col_acc, hidden_state, cell_state, *weights):
        s = Sizes(mesh, params, col_acc, hidden_state, weights[-1])
        return jax.shard_map(
            functools.partial(on_device, s),
            mesh=mesh,
            in_specs=(rowwise, rowwise, P(None, ("fsdp", "rep"), None), P(("fsdp", "rep")), everywhere, everywhere,
                      owned, owned, owned) + (everywhere,) * 5,
            out_specs=(rowwise, P(("fsdp", "rep")), owned, owned, owned),
            check_vma=False,
        )(params, grads, moments, row_acc, lengths, tensor_order, col_acc, hidden_state, cell_state, *weights)

    return step
```

time: 249 us -> 68.1 us (0.27)
  the two profiles are of different devices: /device:TPU:6 before, /device:TPU:1 now
where the time goes in v1:
time: 68.1 us; the launch traced here: 68 us
  Pallas kernels  66.1 us (97%)
  other arithmetic  1.22 us (2%)
    pallas_call x1, Pallas kernels, on_device(): pl.pallas_call(functools.partial(comm_kernel, s), out_shape=(shape((s.rep...  47.2 us
    pallas_call x1, Pallas kernels, on_device(): pl.pallas_call(functools.partial(final_kernel, s), out_shape=(shape(param...  15.7 us
    pallas_call x1, Pallas kernels, on_device(): pl.pallas_call(functools.partial(local_kernel, s), out_shape=(shape((1, r...  3.2 us

profile of v1, /device:TPU:1, one launch (start us, length us, event | category | flops | bytes accessed | tf_op | source)
XLA Modules:
  0.0 68.0 jit_solution(16267487997353840082)
XLA Ops:
  0.6 1.2 %convert_bitcast_fusion = (f32[1,128]{1,0:T(1,128)}, f32[1,128]{1,0:T(1,128)}) fusion(s32[128]{0:T(128)} %param.19, s32[128]{0:T(128)} %param.18), kind=kLoop, calls=%fused_computation | loop fusion | flops 256 | bytes 2048 | tf_op jit(solution)/shard_map/reshape | solution.py:421
  1.9 3.2 %local.1 = (f32[1,48]{1,0:T(1,128)}, f32[48,128]{1,0:T(8,128)}, bf16[8,48,512]{2,1,0:T(8,128)(2,1)}, bf16[2,3712]{1,0:T(2,128)(2,1)}, bf16[2,2,2560]{2,1,0:T(2,128)(2,1)}) custom-call(f32[48,3584]{1,0:T(8,128)} %params.3, bf16[48,3584]{1,0:T(8,128)(2,1)} %grads.3, bf16[3,48,3584]{2,1,0:T(8,128)(2,1)} %moments.3, f32[1,48]{1,0:T(1,128)} %bitcast.8, ...), custom_call_target="tpu_custom_call" | custom-call | tf_op jit(solution)/shard_map/local/pallas_call | solution.py:423
  5.1 47.2 %exchange.1 = (bf16[8,2,3712]{2,1,0:T(2,128)(2,1)}, bf16[2,2,3712]{2,1,0:T(2,128)(2,1)}, bf16[2,8,16,2560]{3,2,1,0:T(8,128)(2,1)}, f32[8,8,512]{2,1,0:T(8,128)}) custom-call(f32[1,128]{1,0:T(1,128)} %get-tuple-element.32.lens, f32[1,128]{1,0:T(1,128)} %get-tuple-element.31.order, bf16[2,3712]{1,0:T(2,128)(2,1)} %get-tuple-element.20.ht, ...), custom_call_target="tpu_custom_call" | custom-call | tf_op jit(solution)/shard_map/exchange/pallas_call | solution.py:437
  52.2 15.7 %networks.1 = (f32[48,3584]{1,0:T(8,128)}, f32[2,3584]{1,0:T(2,128)}, f32[2,512]{1,0:T(2,128)}, f32[2,512]{1,0:T(2,128)}) custom-call(f32[48,3584]{1,0:T(8,128)} %params.3, bf16[48,3584]{1,0:T(8,128)(2,1)} %grads.3, bf16[3,48,3584]{2,1,0:T(8,128)(2,1)} %moments.3, f32[48,128]{1,0:T(8,128)} %get-tuple-element.18.row_var, f32[1,128]{1,0:T(1,128)} %get-tuple-element.32.lens, ...), custom_call_target="tpu_custom_call" | custom-call | tf_op jit(solution)/shard_map/networks/pallas_call | solution.py:455

commit v2 on v1

v2 whole, which is shorter than its diff:
```python
import functools
import math

import jax
import jax.numpy as jnp
from jax import lax
from jax.experimental import pallas as pl
from jax.experimental.pallas import tpu as pltpu
from jax.sharding import PartitionSpec as P

EPS = 1e-06
DECAY = 0.9
FIN = 8
F32 = jnp.float32
BF16 = jnp.bfloat16
MESH = pl.DeviceIdType.MESH
VMEM = pltpu.VMEM
LIMIT = 60 * 1024 * 1024
ANY = pl.BlockSpec(memory_space=pltpu.HBM)


class Sizes:
    def __init__(self, mesh, params, col_acc, hidden_state, rest):
        self.fsdp, self.rep = mesh.shape["fsdp"], mesh.shape["rep"]
        self.nz = self.ny = math.isqrt(self.fsdp)
        self.nt = col_acc.shape[0]
        self.own = self.nt // self.fsdp
        self.rows = params.shape[0] // (self.fsdp * self.rep)
        self.c = params.shape[1]
        self.hid = hidden_state.shape[1]
        self.hm = rest.shape[1] // 4
        self.sl = self.c // (self.rep - 1)
        self.cw = self.c + 128
        self.q = -(-(self.c + 3 * self.hid) // 1024) * 128
        self.all_rows = self.rows + 8
        assert self.own == 2 and self.sl % 128 == 0 and self.rows % 16 == 0


def iota(shape, dim):
    return lax.broadcasted_iota(jnp.int32, shape, dim)


def fiota(shape, dim):
    return iota(shape, dim).astype(F32)


def rem(a, b):
    return lax.rem(a, jnp.int32(b))


def div(a, b):
    return lax.div(a, jnp.int32(b))


def slot_bounds(s, lens, order):
    a, b = iota((s.nt, s.nt), 0), iota((s.nt, s.nt), 1)
    lens_col = jnp.sum(jnp.where(a == b, lens, 0.0), axis=1, keepdims=True)
    ids = a.astype(F32)
    end = jnp.sum(jnp.where(ids <= order, lens_col, 0.0), axis=0, keepdims=True)
    size = jnp.sum(jnp.where(ids == order, lens_col, 0.0), axis=0, keepdims=True)
    return end - size, end


def slot_hits(pos, start, end):
    return jnp.where((pos >= start) & (pos < end), 1.0, 0.0)


def ranges(pos, start, end):
    hits = slot_hits(pos, start, end)
    first = jnp.sum(hits * start, axis=1, keepdims=True)
    last = jnp.sum(hits * end, axis=1, keepdims=True)
    return first, last, hits


def split2(x):
    hi = x.astype(BF16)
    return hi, (x - hi.astype(F32)).astype(BF16)


def restack(t):
    lane = iota(t.shape, 1)
    both = t + pltpu.roll(t, 120, 1)
    hi = both.astype(BF16).astype(F32)
    low = pltpu.roll(both - hi, 8, 1)
    return jnp.where(lane < 8, hi, jnp.where(lane < 16, low, 0.0))


def remote(src, dst, send_sem, recv_sem, fsdp, rep):
    return pltpu.make_async_remote_copy(
        src_ref=src, dst_ref=dst, send_sem=send_sem, recv_sem=recv_sem,
        device_id={"fsdp": fsdp, "rep": rep}, device_id_type=MESH,
    )


def log_features(means, col_mean, col_square):
    feats = [jnp.log(means[k] + EPS) for k in range(5)]
    feats += [means[5] / jnp.sqrt(means[0] * means[1] + EPS), means[6] / jnp.sqrt(means[0] * means[3] + EPS),
              means[7] / jnp.sqrt(means[1] * means[3] + EPS), jnp.log(col_mean + EPS),
              jnp.log(col_square / (col_mean * col_mean))]
    return [v.astype(BF16).astype(F32) for v in feats]


def cell_step(s, feats, rec, w_in, bias, old):
    def gate(k):
        lo, hi = k * s.hid, (k + 1) * s.hid
        out = rec(k) + bias[:, lo:hi]
        w = w_in[:, lo:hi].astype(F32)
        for i, v in enumerate(feats):
            out = out + v * w[i : i + 1]
        return out

    now = jax.nn.sigmoid(gate(1)) * old + jax.nn.sigmoid(gate(0)) * jnp.tanh(gate(2))
    return jax.nn.sigmoid(gate(3)) * jnp.tanh(now), now


def kernel(s, params_h, grads_h, moments_h, row_acc_h, lens_h, order_h, col_acc_h, hidden_h, cell_h, w_in_h, w_rec_h,
           bias_h, w_first_h, w_rest_h,
           update_h, row_new_h, col_new_h, hidden_new_h, cell_new_h,
           params, grads, moments, row_acc, lens_i, order_i, col_acc, hidden, cell, w_in, w_rec, bias, w_first, w_rest,
           s_in, s_big, s_w, s_out,
           gs, ht, ag, htall, nb, table, nbsrc, gx, zsrc, zbuf, ysrc, ybuf,
           sent, one_come, p_come, t_come, y_come,
           cols, ht16, gen, scales, pick_w2, own_rec, held, update, row_new, col_new, hidden_new, cell_new):
    f, r = lax.axis_index("fsdp"), lax.axis_index("rep")
    z, y, core = div(f, s.ny), rem(f, s.ny), rem(r, 2)
    partner = r + 1 - 2 * core
    nxt, prv = rem(f + 1, s.fsdp), rem(f + s.fsdp - 1, s.fsdp)
    rows, nt, chunks, per = s.rows, s.nt, s.rep - 1, 2 * s.ny
    reps, ys, zs = range(1, s.rep), range(1, s.ny), range(1, s.nz)

    def at_rep(k):
        return rem(r + k, s.rep)

    def at_y(k):
        return z * s.ny + rem(y + k, s.ny)

    def at_z(k):
        return rem(z + k, s.nz) * s.ny + y

    ht_k, g_k, z_k, d_k, nb_k, p_k, t_k, y_k, y0_k = range(9)

    def all_come(ref, kind, fsdp, rep):
        remote(ref, ref, sent.at[kind], one_come.at[kind], fsdp, rep).wait_recv()

    def first_axis(k):
        return (1 - core) * at_y(k) + core * at_z(k)

    def second_axis(k):
        return (1 - core) * at_z(k) + core * at_y(k)

    with jax.named_scope("greet"):
        def fetch(pairs, sem):
            made = [pltpu.make_async_copy(a, b, sem.at[i]) for i, (a, b) in enumerate(pairs)]
            for c in made:
                c.start()
            return made

        small = fetch([(col_acc_h, col_acc), (hidden_h, hidden), (cell_h, cell), (lens_h, lens_i), (order_h, order_i),
                       (row_acc_h, row_acc)], s_in)
        barrier = pltpu.get_barrier_semaphore()
        peers = [(at_z(k), 2 * x) for k in zs for x in range(s.rep // 2)]
        peers += [(at_y(k), 2 * x + 1) for k in ys for x in range(s.rep // 2)]
        peers += [(f, at_rep(k)) for k in reps] + [(first_axis(k), r) for k in ys] + [(nxt, r), (prv, r)]
        for pf, pr in peers:
            pl.semaphore_signal(barrier, inc=1, device_id={"fsdp": pf, "rep": pr}, device_id_type=MESH)
        big = fetch([(grads_h, grads)] + [(moments_h.at[k], moments.at[k]) for k in range(3)] + [(params_h, params)], s_big)
        weights = fetch([(w_rec_h, w_rec), (w_in_h, w_in), (bias_h, bias), (w_first_h, w_first), (w_rest_h, w_rest)], s_w)

    with jax.named_scope("own"):
        for c in small[:3]:
            c.wait()
        own = jnp.concatenate([v.astype(BF16) for v in (col_acc[...], hidden[...])] + list(split2(cell[...])), axis=1)
        if s.c + 3 * s.hid < 8 * s.q:
            own = jnp.concatenate([own, jnp.zeros((2, 8 * s.q - s.c - 3 * s.hid), BF16)], axis=1)
        own = own.astype(F32)
        for half in range(2):
            parts = [own[:, (4 * half + q) * s.q : (4 * half + q + 1) * s.q] for q in range(4)]
            ag[half] = jnp.concatenate(parts, axis=0).astype(BF16)
    with jax.named_scope("meet"):
        pl.semaphore_wait(barrier, len(peers))
        c_p = {k: remote(ag.at[core], table.at[core, 0, k], sent.at[p_k], p_come.at[k], first_axis(k), r) for k in ys}
        near = sorted(zs, key=lambda k: min(k, s.nz - k))
        ring = s.nz == 8
        early = (0, 1, 7, 2, 6) if ring else ()
        t_two = {}

        def hop(src, slot, piece, to):
            sem = t_come.at[8 + 2 * piece + (slot == 6)] if slot in (2, 6) and piece in early else t_come.at[slot]
            c = remote(src, table.at[core, slot, piece], sent.at[t_k], sem, second_axis(to), r)
            c.start()
            return c

        def pass_on(piece, src):
            for k in (2, 6, 1, 7) if piece in early else near[::-1]:
                t_two[k, piece] = hop(src, k, piece, k)

        def relay(piece):
            t_two[2, piece].wait_recv()
            if piece % 2 == 0:
                hop(table.at[core, 2, piece], 4, piece, 2)
            hop(table.at[core, 2, piece], 3, piece, 1)
            t_two[6, piece].wait_recv()
            if piece % 2 == 1:
                hop(table.at[core, 6, piece], 4, piece, 6)
            hop(table.at[core, 6, piece], 5, piece, 7)

        for k in near[::-1]:
            c_p[k].start()
        pass_on(0, ag.at[core])
        table[core, 0, 0] = ag[core]

    with jax.named_scope("stats"):
        for c in big:
            c.wait()
        sums = [jnp.zeros((rows, 1), F32) for _ in range(8)]
        for j in range(chunks):
            cs = pl.ds(j * s.sl, s.sl)
            g, p = grads[:, cs].astype(F32), params[:, cs]
            m = [moments[k, :, cs].astype(F32) for k in range(3)]
            sq = g * g
            gs[j] = sq.astype(BF16)
            for k, v in enumerate((sq, m[0] * m[0], m[1] * m[1], m[2] * m[2], p * p, g * m[0], g * m[2], m[0] * m[2])):
                sums[k] = sums[k] + jnp.sum(v, axis=1, keepdims=True)
        lane = iota((rows, 128), 1)
        stats = jnp.zeros((rows, 128), F32)
        for k in range(8):
            hi, low = split2(sums[k])
            stats = jnp.where(lane == k, hi.astype(F32), stats)
            stats = jnp.where(lane == k + 8, low.astype(F32), stats)
        gs[chunks] = jnp.zeros((rows, s.sl), BF16)
        gs[chunks, :, :128] = stats.astype(BF16)
    with jax.named_scope("send1"):
        c_g = [remote(gs.at[at_rep(k)], gx.at[k], sent.at[g_k], one_come.at[g_k], f, at_rep(k)) for k in reps]
        for c in c_g:
            c.start()
    with jax.named_scope("ends"):
        for c in small[3:]:
            c.wait()
        lens, order = lens_i[...].astype(F32), order_i[...].astype(F32)
        start, end = slot_bounds(s, lens, order)
        base = ((f * s.rep + r) * rows).astype(F32)
        which = fiota((16, 1), 0)
        pos = jnp.where(which == 0.0, base, jnp.where(which == 1.0, base + (rows - 1), -1.0))
        first, last, _ = ranges(pos, start, end)
        here = base + fiota((1, rows), 1)
        pick = slot_hits(here, first, last).astype(BF16)
        for j in range(chunks):
            part = jnp.dot(pick, gs[j], preferred_element_type=F32)
            ht[:, j * s.sl : (j + 1) * s.sl] = part[:2].astype(BF16)
        part = jnp.dot(pick, gs[chunks, :, :128], preferred_element_type=F32)
        ht[:, s.c :] = restack(part)[:2].astype(BF16)
        c_ht = [remote(ht, htall.at[k], sent.at[ht_k], one_come.at[ht_k], f, at_rep(k)) for k in reps]
        for c in c_ht:
            c.start()
        htall[0] = ht[...]
        gx[0] = gs[r]
        a, b = iota((rows, rows), 0), iota((rows, rows), 1)
        acc_col = jnp.sum(jnp.where(a == b, row_acc[...], 0.0), axis=1, keepdims=True)
        new_col = DECAY * acc_col + (1.0 - DECAY) * (sums[0] / s.c)
        row_new[...] = jnp.sum(jnp.where(a == b, new_col, 0.0), axis=0, keepdims=True)
        scales[:, 4:5] = new_col

    group = (f * (s.rep * rows)).astype(F32)
    which = fiota((8, 1), 0)
    first, last, _ = ranges(jnp.where(which == 0.0, group + (s.rep * rows - 1), group), start, end)
    coef = []
    for k in range(s.rep):
        at = group + (rem(r + s.rep - k, s.rep) * rows).astype(F32)
        head = jnp.where((at >= first) & (at < last), 1.0, 0.0)
        tail = jnp.where((at + (rows - 1) >= first) & (at + (rows - 1) < last), 1.0, 0.0)
        coef.append((head, tail * (1.0 - head)))

    width, m, taps = (FIN + 4) * s.hm, 8 * s.hm, 8 * (FIN + 2)
    lw = iota((m, width), 1)
    spread = jnp.where(rem(iota((m, 8), 0), 8) == iota((m, 8), 1), 1.0, 0.0).astype(BF16)
    keep = (rem(lw, s.hm) == div(iota((m, width), 0), 8)) & (lw < (FIN + 1) * s.hm)
    fold = jnp.where(div(iota((width, taps), 0), s.hm) == div(iota((width, taps), 1), 8), 1.0, 0.0).astype(BF16)
    diag1 = (rem(iota((m, taps), 0), 8) == rem(iota((m, taps), 1), 8)) & (iota((m, taps), 1) < 8 * (FIN + 1))
    diag2 = iota((8, m), 0) == rem(iota((8, m), 1), 8)
    for o in range(3):
        want = (FIN + 1) * s.hm + 3 * div(iota((width, m), 1), 8) + o
        pick_w2[o] = jnp.where(iota((width, m), 0) == want, 1.0, 0.0).astype(BF16)

    with jax.named_scope("wait_p"):
        then = {6: (0,), 5: (1, 7), 4: (2, 6)} if ring else {}
        for k in near:
            c_p[k].wait_recv()
            pass_on(k, table.at[core, 0, k])
            for piece in then.get(k, ()):
                relay(piece)
        c_d = [remote(table.at[core, k], table.at[core, k], sent.at[d_k], one_come.at[d_k], f, partner) for k in range(s.nz)]
        c_d[0].start()
    with jax.named_scope("wait_g"):
        a, b = iota((nt, nt), 0), iota((nt, nt), 1)
        k1, p2, j2 = div(a, per), rem(div(a, 2), s.nz), rem(a, 2)
        slot = (1 - core) * (p2 * per + rem(y + k1, s.ny) * 2 + j2) + core * (rem(z + k1, s.nz) * per + p2 * 2 + j2)
        order_col = jnp.sum(jnp.where(b == slot, order, 0.0), axis=1, keepdims=True)
        ids = b.astype(F32)
        end_col = jnp.sum(jnp.where(ids <= order_col, lens, 0.0), axis=1, keepdims=True)
        start_col = end_col - jnp.sum(jnp.where(ids == order_col, lens, 0.0), axis=1, keepdims=True)
        all_come(gx.at[pl.ds(1, s.rep - 1)], g_k, f, r)
        part = jnp.zeros((nt, s.sl), F32)
        for k in range(s.rep):
            at = group + (rem(r + s.rep - k, s.rep) * rows).astype(F32) + fiota((1, rows), 1)
            part = part + jnp.dot(slot_hits(at, start_col, end_col).astype(BF16), gx[k], preferred_element_type=F32)
        for k in range(s.nz):
            zsrc[k] = part[k * per : (k + 1) * per].astype(BF16)
        c_z = [remote(zsrc.at[k], zbuf.at[k], sent.at[z_k], one_come.at[z_k], first_axis(k), r) for k in zs]
        for c in c_z:
            c.start()
        zbuf[0] = zsrc[0]
    with jax.named_scope("wait_ht"):
        all_come(htall.at[pl.ds(1, s.rep - 1)], ht_k, f, r)
        acc = jnp.zeros((2, s.cw), F32)
        for k in range(s.rep):
            both = htall[k].astype(F32)
            acc = acc + coef[k][0][:2] * both[0:1] + coef[k][1][:2] * both[1:2]
            ht16[2 * k : 2 * k + 2, :] = both
        acc = jnp.concatenate([acc[:, : s.c], restack(acc[:, s.c :])], axis=1)
        nbsrc[0] = jnp.broadcast_to(acc[0:1], (2, s.cw)).astype(BF16)
        nbsrc[1] = jnp.broadcast_to(acc[1:2], (2, s.cw)).astype(BF16)
        c_nb = [remote(nbsrc.at[i], nb.at[i], sent.at[nb_k], one_come.at[nb_k + 4 + i], to, r) for i, to in enumerate((nxt, prv))]
        for c in c_nb:
            c.start()

    n = s.all_rows
    row = iota((n, 1), 0)
    pos = jnp.where(row < rows, base + row.astype(F32), -1.0)
    lane = iota((n, nt), 1)
    hits = slot_hits(pos, start, end)
    hits = hits + jnp.where((row >= rows) & (row < rows + 2) & (lane == row - rows + 2 * f), 1.0, 0.0)
    first = jnp.sum(hits * start, axis=1, keepdims=True)
    last = jnp.sum(hits * end, axis=1, keepdims=True)
    length = jnp.maximum(last - first, 1.0)
    slot_of = jnp.sum(hits * lane.astype(F32), axis=1, keepdims=True)[:rows]
    first, last = first[:rows], last[:rows]
    same = slot_hits(base + fiota((1, rows), 1), first, last).astype(BF16)
    la = iota((1, 2 * s.rep), 1)
    head = group + (rem(r + s.rep - div(la, 2), s.rep) * rows).astype(F32)
    in_head = slot_hits(head, first, last)
    in_tail = slot_hits(head + (rows - 1), first, last) * (1.0 - in_head)
    shared = jnp.where(div(la, 2) == 0, 0.0, jnp.where(rem(la, 2) == 0, in_head, in_tail)).astype(BF16)
    before = slot_hits(group - 1.0, first, last)
    after = slot_hits(group + s.rep * rows, first, last)
    deep = s.nz * s.ny * 8
    lane = iota((rows, deep), 1)
    k2, k1, q4, j2 = div(lane, 8 * s.ny), rem(div(lane, 8), s.ny), rem(div(lane, 2), 4), rem(lane, 2)
    picks = []
    for half in range(2):
        kz, ky = (k2, k1) if half == 0 else (k1, k2)
        slot = rem(z + s.nz - kz, s.nz) * per + rem(y + s.ny - ky, s.ny) * 2 + j2
        hit = slot.astype(F32) == slot_of
        picks.append(jnp.concatenate([jnp.where(hit & (q4 == q), 1.0, 0.0) for q in range(4)], axis=0).astype(BF16))
    top = iota((8, 1), 0)

    def own_rows(v):
        return jnp.where(top == 0, v[0:1], jnp.where(top == 1, v[1:2], 0.0))

    def full_sums(g, lo, hi):
        out = jnp.dot(same, g, preferred_element_type=F32)
        out = out + jnp.dot(shared, ht16[:, lo:hi].astype(BF16), preferred_element_type=F32)
        return out + before * nb[0, :, lo:hi].astype(F32)[0:1] + after * nb[1, :, lo:hi].astype(F32)[0:1]

    with jax.named_scope("wait_t"):
        for k in near:
            ref = table.at[core, k, pl.ds(3, 3)] if ring and k in (2, 6) else table.at[core, k]
            remote(ref, ref, sent.at[t_k], t_come.at[k], f, r).wait_recv()
            c_d[k].start()
    with jax.named_scope("wait_z"):
        all_come(zbuf.at[pl.ds(1, s.nz - 1)], z_k, f, r)
        total = zbuf[0].astype(F32)
        for k in zs:
            total = total + zbuf[k].astype(F32)
        total = total.astype(BF16)
        for k in range(s.ny):
            ysrc[k] = total[2 * k : 2 * k + 2]
        second = (1 - core) * z + core * y
        c_y = []
        for a in range(s.ny):
            for b in range(s.rep):
                if a or b:
                    c_y.append(remote(ysrc.at[rem(second + a, s.ny)], ybuf.at[a, r], sent.at[y_k if a else y0_k],
                                      y_come.at[a if a else s.ny + b], second_axis(a), at_rep(b)))
        for c in c_y:
            c.start()
        ybuf[0, r] = ysrc[second]

    with jax.named_scope("wait_d"):
        for c in c_nb:
            c.wait_recv()
        all_come(table.at[1 - core], d_k, f, partner)

    with jax.named_scope("rows"):
        for half in range(2):
            got = jnp.dot(picks[half], table[half].reshape(deep, s.q), preferred_element_type=F32)
            for q in range(4):
                held[:, (4 * half + q) * s.q : (4 * half + q + 1) * s.q] = got[q * rows : (q + 1) * rows]
        total_col = jnp.zeros((rows, 1), F32)
        total_sq = jnp.zeros((rows, 1), F32)
        size = length[:rows]
        for j in range(chunks):
            lo, hi = j * s.sl, (j + 1) * s.sl
            new = DECAY * held[:, lo:hi] + (1.0 - DECAY) * full_sums(gs[j], lo, hi) / size
            cols[:, lo:hi] = new
            total_col = total_col + jnp.sum(new, axis=1, keepdims=True)
            total_sq = total_sq + jnp.sum(new * new, axis=1, keepdims=True)
        stats = full_sums(gs[chunks, :, :128], s.c, s.cw)
        means = [(stats[:, k : k + 1] + stats[:, k + 8 : k + 9]) / (size * s.c) for k in range(8)]
        col_mean = total_col / s.c
        feats = log_features(means, col_mean, total_sq / s.c)
        for c in weights:
            c.wait()
        hid = jnp.concatenate([held[:, s.c : s.c + s.hid], own_rows(hidden[...])], axis=0).astype(BF16)
        old = held[:, s.c + s.hid : s.c + 2 * s.hid] + held[:, s.c + 2 * s.hid : s.c + 3 * s.hid]

        def rec(k):
            out = jnp.dot(hid, w_rec[:, k * s.hid : (k + 1) * s.hid], preferred_element_type=F32)
            own_rec[k] = out[rows:]
            return out[:rows]

        state, _ = cell_step(s, feats, rec, w_in, bias, old)
        bf = state.astype(BF16)
        gen[:, : FIN * s.hm] = jnp.dot(bf, w_first[...], preferred_element_type=F32)
        gen[:, FIN * s.hm :] = jnp.dot(bf, w_rest[...], preferred_element_type=F32)
        scales[:, 0:1] = scales[:, 4:5] / col_mean
        for i, k in enumerate((0, 1, 4)):
            scales[:, i + 1 : i + 2] = 1.0 / jnp.sqrt(means[k] + EPS)

    wide = s.c // 2 if s.c % 256 == 0 else s.c
    ones, zeros = jnp.ones((8, wide), F32), jnp.zeros((8, wide), F32)

    blocks = rows // 16
    outs = []

    def block(i):
        at = 16 * i
        made = gen[at : at + 16, :].astype(BF16).astype(F32)
        sc = scales[at : at + 16, :]
        nets = []
        for half in range(2):
            mine = made[8 * half : 8 * half + 8].astype(BF16)
            y1 = jnp.where(keep, jnp.dot(spread, mine, preferred_element_type=F32), 0.0).astype(BF16)
            w1 = jnp.where(diag1, jnp.dot(y1, fold, preferred_element_type=F32), 0.0).astype(BF16)
            w2 = [jnp.where(diag2, jnp.dot(mine, pick_w2[o], preferred_element_type=F32), 0.0) for o in range(3)]
            nets.append((w1, jnp.concatenate(w2, axis=0).astype(BF16)))
        for j in range(s.c // wide):
            lo, hi = j * wide, (j + 1) * wide
            g16 = grads[at : at + 16, lo:hi].astype(F32)
            m16 = [moments[k, at : at + 16, lo:hi].astype(F32) for k in range(3)]
            p16 = params[at : at + 16, lo:hi]
            c16 = cols[at : at + 16, lo:hi]
            for half in range(2):
                q = slice(8 * half, 8 * half + 8)
                g, m0, m1, m2, p, cn = g16[q], m16[0][q], m16[1][q], m16[2][q], p16[q], c16[q]
                rms = lax.rsqrt(cn * sc[q, 0:1] + EPS)
                gn, mn = g * rms, m0 * rms
                x = jnp.concatenate(
                    [gn, mn, m1 * rms, m2 * rms, g * sc[q, 1:2], m0 * sc[q, 2:3], p * sc[q, 3:4], gn * mn, ones, zeros],
                    axis=0,
                ).astype(BF16)
                w1, w2 = nets[half]
                unit = jnp.maximum(jnp.dot(w1, x, preferred_element_type=F32), 0.0).astype(BF16)
                o = jnp.dot(w2, unit, preferred_element_type=F32)
                out = o[0:8] * jnp.exp(jnp.tanh(o[8:16])) * jax.nn.sigmoid(o[16:24])
                update[at + 8 * half : at + 8 * half + 8, lo:hi] = out

        c = pltpu.make_async_copy(update.at[pl.ds(at, 16)], update_h.at[pl.ds(at, 16)], s_out.at[i])
        c.start()
        outs.append(c)

    def owners():
        for a in ys:
            remote(ybuf.at[a], ybuf.at[a], sent.at[y_k], y_come.at[a], f, r).wait_recv()
        for c in c_y[: s.rep - 1]:
            c.wait_recv()
        size = length[rows:]

        def arrived(j):
            t = ybuf[0, j].astype(F32)
            for a in range(1, s.ny):
                t = t + ybuf[a, j].astype(F32)
            return own_rows(t)

        total_col = jnp.zeros((8, 1), F32)
        total_sq = jnp.zeros((8, 1), F32)
        for j in range(chunks):
            lo, hi = j * s.sl, (j + 1) * s.sl
            new = DECAY * own_rows(col_acc[:, lo:hi]) + (1.0 - DECAY) * arrived(j) / size
            col_new[:, lo:hi] = new[:2]
            total_col = total_col + jnp.sum(new, axis=1, keepdims=True)
            total_sq = total_sq + jnp.sum(new * new, axis=1, keepdims=True)
        stats = arrived(chunks)[:, :128]
        means = [(stats[:, k : k + 1] + stats[:, k + 8 : k + 9]) / (size * s.c) for k in range(8)]
        feats = log_features(means, total_col / s.c, total_sq / s.c)
        state, now = cell_step(s, feats, lambda k: own_rec[k], w_in, bias, own_rows(cell[...]))
        hidden_new[...] = state[:2]
        cell_new[...] = now[:2]
        for i, (a, b) in enumerate(((row_new, row_new_h), (col_new, col_new_h), (hidden_new, hidden_new_h), (cell_new, cell_new_h))):
            c = pltpu.make_async_copy(a, b, s_out.at[blocks + i])
            c.start()
            outs.append(c)

    for i in range(blocks):
        with jax.named_scope("block"):
            block(i)
    with jax.named_scope("owners"):
        owners()
    with jax.named_scope("drain"):
        def all_sent(ref, kind):
            remote(ref, ref, sent.at[kind], one_come.at[kind], f, r).wait_send()

        some, others = pl.ds(1, s.rep - 1), pl.ds(1, s.nz - 1)
        all_sent(htall.at[some], ht_k)
        all_sent(gx.at[some], g_k)
        all_sent(zbuf.at[others], z_k)
        all_sent(table.at[core], d_k)
        all_sent(nb, nb_k)
        all_sent(table.at[core, 0, others], p_k)
        all_sent(table.at[core, others], t_k)
        all_sent(ybuf.at[others], y_k)
        all_sent(ybuf.at[0, some], y0_k)
        for c in outs:
            c.wait()


def put_out(*refs):
    here, there, held, sems = refs[:5], refs[5:10], refs[10:15], refs[15]
    come = [pltpu.make_async_copy(a, b, sems.at[0, i]) for i, (a, b) in enumerate(zip(here, held))]
    go = [pltpu.make_async_copy(a, b, sems.at[1, i]) for i, (a, b) in enumerate(zip(held, there))]
    for c in come:
        c.start()
    for a, b in zip(come, go):
        a.wait()
        b.start()
    for c in go:
        c.wait()


def on_device(s, params, grads, moments, row_acc, lengths, tensor_order, col_acc, hidden_state, cell_state,
              lstm_in, lstm_rec, lstm_bias, hyper_first, hyper_rest):
    shape = jax.ShapeDtypeStruct
    rows, per, width = s.rows, 2 * s.ny, (FIN + 4) * s.hm
    args = (params, grads, moments, row_acc.reshape(1, rows), lengths.reshape(1, s.nt), tensor_order.reshape(1, s.nt),
            col_acc, hidden_state, cell_state, lstm_in, lstm_rec, lstm_bias.reshape(1, -1), hyper_first, hyper_rest)

    def sems(k):
        return pltpu.SemaphoreType.DMA((2, k))

    def one(k):
        return pltpu.SemaphoreType.DMA((k,))

    outs = (
        shape(params.shape, F32), shape((1, rows), F32), shape(col_acc.shape, F32), shape(hidden_state.shape, F32),
        shape(cell_state.shape, F32),
    )
    made = pl.pallas_call(
        functools.partial(kernel, s),
        out_shape=outs,
        in_specs=[ANY] * len(args),
        out_specs=(ANY,) * 5,
        scratch_shapes=[VMEM(a.shape, a.dtype) for a in args] + [
            one(6), one(5), one(5), one(rows // 16 + 4),
            VMEM((s.rep, rows, s.sl), BF16), VMEM((2, s.cw), BF16), VMEM((2, 8, s.q), BF16),
            VMEM((s.rep, 2, s.cw), BF16), VMEM((2, 2, s.cw), BF16), VMEM((2, s.nz, s.ny, 8, s.q), BF16),
            VMEM((2, 2, s.cw), BF16), VMEM((s.rep, rows, s.sl), BF16),
            VMEM((s.nz, per, s.sl), BF16), VMEM((s.nz, per, s.sl), BF16), VMEM((s.ny, 2, s.sl), BF16),
            VMEM((s.ny, s.rep, 2, s.sl), BF16),
            one(9), one(10), one(s.ny), one(8 + 2 * s.ny), one(s.ny + s.rep),
            VMEM((rows, s.c), F32), VMEM((2 * s.rep, s.cw), F32), VMEM((rows, width), F32), VMEM((rows, 128), F32),
            VMEM((3, width, 8 * s.hm), BF16), VMEM((4, 8, s.hid), F32),
            VMEM((rows, 8 * s.q), F32),
        ] + [VMEM(o.shape, o.dtype) for o in outs],
        compiler_params=pltpu.CompilerParams(collective_id=0, has_side_effects=True, vmem_limit_bytes=LIMIT),
        name="step",
    )(*args)
    update, row_new, col_new, hidden_new, cell_new = pl.pallas_call(
        put_out,
        out_shape=outs,
        in_specs=[ANY] * 5,
        out_specs=(ANY,) * 5,
        scratch_shapes=[VMEM(o.shape, o.dtype) for o in outs] + [sems(5)],
        compiler_params=pltpu.CompilerParams(vmem_limit_bytes=LIMIT),
        name="out",
    )(*made)
    return update, row_new.reshape(rows), col_new, hidden_new, cell_new


def solution(mesh):
    rowwise, owned, everywhere = P(("fsdp", "rep"), None), P("fsdp", None), P()

    def step(params, grads, moments, row_acc, lengths, tensor_order, col_acc, hidden_state, cell_state, *weights):
        s = Sizes(mesh, params, col_acc, hidden_state, weights[-1])
        return jax.shard_map(
            functools.partial(on_device, s),
            mesh=mesh,
            in_specs=(rowwise, rowwise, P(None, ("fsdp", "rep"), None), P(("fsdp", "rep")), everywhere, everywhere,
                      owned, owned, owned) + (everywhere,) * 5,
            out_specs=(rowwise, P(("fsdp", "rep")), owned, owned, owned),
            check_vma=False,
        )(params, grads, moments, row_acc, lengths, tensor_order, col_acc, hidden_state, cell_state, *weights)

    return step
```

time: 68.1 us -> 43.6 us (0.64)
  Pallas kernels: 66.1 us -> 42.7 us
  other arithmetic: 1.22 us -> 0 us
    pallas_call x3 -> x2, Pallas kernels: 66.1 us -> 42.7 us  [the longest x1 40.7 us: on_device(): pl.pallas_call(functools.partial(kernel, s), out_shape=outs, in_specs=[AN...]
    reshape x1 -> x0, other arithmetic: 1.22 us -> none  [on_device(): order = tensor_order.astype(F32).reshape(1, s.nt)]
where the time goes in v2:
time: 43.6 us; the launch traced here: 43.4 us
  Pallas kernels  42.7 us (98%)
  between operations  0.65 us (1%)
    pallas_call x1, Pallas kernels, on_device(): pl.pallas_call(functools.partial(kernel, s), out_shape=outs, in_specs=[AN...  40.7 us
    pallas_call x1, Pallas kernels, on_device(): pl.pallas_call(put_out, out_shape=outs, in_specs=[ANY] * 5, out_specs=(AN...  2.04 us

profile of v2, /device:TPU:1, one launch (start us, length us, event | category | flops | bytes accessed | tf_op | source)
XLA Modules:
  0.0 43.4 jit_solution(1862872236816009553)
XLA Ops:
  0.6 40.7 %step.1 = (f32[48,3584]{1,0:T(8,128)}, f32[1,48]{1,0:T(1,128)}, f32[2,3584]{1,0:T(2,128)}, f32[2,512]{1,0:T(2,128)}, f32[2,512]{1,0:T(2,128)}) custom-call(f32[48,3584]{1,0:T(8,128)} %params_h.1, bf16[48,3584]{1,0:T(8,128)(2,1)} %grads_h.1, bf16[3,48,3584]{2,1,0:T(8,128)(2,1)} %moments_h.1, f32[1,48]{1,0:T(1,128)} %bitcast.6, s32[1,128]{1,0:T(1,128)} %bitcast.7, ...), custom_call_target="tpu_custom_call" | custom-call | tf_op jit(solution)/shard_map/step/pallas_call | solution.py:556
  41.4 2.0 %out.1 = (f32[48,3584]{1,0:T(8,128)}, f32[1,48]{1,0:T(1,128)}, f32[2,3584]{1,0:T(2,128)}, f32[2,512]{1,0:T(2,128)}, f32[2,512]{1,0:T(2,128)}) custom-call(f32[48,3584]{1,0:T(8,128)} %get-tuple-element.15.refs_0_, f32[1,48]{1,0:T(1,128)} %get-tuple-element.16.refs_1_, f32[2,3584]{1,0:T(2,128)} %get-tuple-element.17.refs_2_, ...), custom_call_target="tpu_custom_call" | custom-call | tf_op jit(solution)/shard_map/out/pallas_call | solution.py:576

commit v3 on v2

--- a/solution.py
+++ b/solution.py
@@ -120,7 +120,7 @@
            s_in, s_big, s_w, s_out,
            gs, ht, ag, htall, nb, table, nbsrc, gx, zsrc, zbuf, ysrc, ybuf,
            sent, one_come, p_come, t_come, y_come,
-           cols, ht16, gen, scales, pick_w2, own_rec, held, update, row_new, col_new, hidden_new, cell_new):
+           cols, ht16, gen, scales, pick_w2, net1, net2, own_rec, held, update, row_new, col_new, hidden_new, cell_new):
     f, r = lax.axis_index("fsdp"), lax.axis_index("rep")
     z, y, core = div(f, s.ny), rem(f, s.ny), rem(r, 2)
     partner = r + 1 - 2 * core
@@ -157,14 +157,15 @@
 
         small = fetch([(col_acc_h, col_acc), (hidden_h, hidden), (cell_h, cell), (lens_h, lens_i), (order_h, order_i),
                        (row_acc_h, row_acc)], s_in)
+        big = fetch([(grads_h, grads)] + [(moments_h.at[k], moments.at[k]) for k in range(3)] + [(params_h, params)], s_big)
         barrier = pltpu.get_barrier_semaphore()
         peers = [(at_z(k), 2 * x) for k in zs for x in range(s.rep // 2)]
         peers += [(at_y(k), 2 * x + 1) for k in ys for x in range(s.rep // 2)]
         peers += [(f, at_rep(k)) for k in reps] + [(first_axis(k), r) for k in ys] + [(nxt, r), (prv, r)]
         for pf, pr in peers:
             pl.semaphore_signal(barrier, inc=1, device_id={"fsdp": pf, "rep": pr}, device_id_type=MESH)
-        big = fetch([(grads_h, grads)] + [(moments_h.at[k], moments.at[k]) for k in range(3)] + [(params_h, params)], s_big)
-        weights = fetch([(w_rec_h, w_rec), (w_in_h, w_in), (bias_h, bias), (w_first_h, w_first), (w_rest_h, w_rest)], s_w)
+    def fetch_weights():
+        return fetch([(w_rec_h, w_rec), (w_in_h, w_in), (bias_h, bias), (w_first_h, w_first), (w_rest_h, w_rest)], s_w)
 
     with jax.named_scope("own"):
         for c in small[:3]:
@@ -233,6 +234,7 @@
         c_g = [remote(gs.at[at_rep(k)], gx.at[k], sent.at[g_k], one_come.at[g_k], f, at_rep(k)) for k in reps]
         for c in c_g:
             c.start()
+        weights = fetch_weights()
     with jax.named_scope("ends"):
         for c in small[3:]:
             c.wait()
@@ -282,14 +284,12 @@
         pick_w2[o] = jnp.where(iota((width, m), 0) == want, 1.0, 0.0).astype(BF16)
 
     with jax.named_scope("wait_p"):
-        then = {6: (0,), 5: (1, 7), 4: (2, 6)} if ring else {}
+        then = {6: (0,)} if ring else {}
         for k in near:
             c_p[k].wait_recv()
             pass_on(k, table.at[core, 0, k])
             for piece in then.get(k, ()):
                 relay(piece)
-        c_d = [remote(table.at[core, k], table.at[core, k], sent.at[d_k], one_come.at[d_k], f, partner) for k in range(s.nz)]
-        c_d[0].start()
     with jax.named_scope("wait_g"):
         a, b = iota((nt, nt), 0), iota((nt, nt), 1)
         k1, p2, j2 = div(a, per), rem(div(a, 2), s.nz), rem(a, 2)
@@ -309,6 +309,11 @@
         for c in c_z:
             c.start()
         zbuf[0] = zsrc[0]
+    with jax.named_scope("relay"):
+        for piece in (1, 7, 2, 6) if ring else ():
+            relay(piece)
+        c_d = [remote(table.at[core, k], table.at[core, k], sent.at[d_k], one_come.at[d_k], f, partner) for k in range(s.nz)]
+        c_d[0].start()
     with jax.named_scope("wait_ht"):
         all_come(htall.at[pl.ds(1, s.rep - 1)], ht_k, f, r)
         acc = jnp.zeros((2, s.cw), F32)
@@ -361,11 +366,23 @@
         out = out + jnp.dot(shared, ht16[:, lo:hi].astype(BF16), preferred_element_type=F32)
         return out + before * nb[0, :, lo:hi].astype(F32)[0:1] + after * nb[1, :, lo:hi].astype(F32)[0:1]
 
+    def got_block(k):
+        ref = table.at[core, k, pl.ds(3, 3)] if ring and k in (2, 6) else table.at[core, k]
+        remote(ref, ref, sent.at[t_k], t_come.at[k], f, r).wait_recv()
+        c_d[k].start()
+
     with jax.named_scope("wait_t"):
         for k in near:
-            ref = table.at[core, k, pl.ds(3, 3)] if ring and k in (2, 6) else table.at[core, k]
-            remote(ref, ref, sent.at[t_k], t_come.at[k], f, r).wait_recv()
-            c_d[k].start()
+            got_block(k)
+    with jax.named_scope("wait_nb"):
+        for c in c_nb:
+            c.wait_recv()
+        size = length[:rows]
+        for j in range(chunks):
+            lo, hi = j * s.sl, (j + 1) * s.sl
+            cols[:, lo:hi] = full_sums(gs[j], lo, hi) * ((1.0 - DECAY) / size)
+        stats = full_sums(gs[chunks, :, :128], s.c, s.cw)
+        means = [(stats[:, k : k + 1] + stats[:, k + 8 : k + 9]) / (size * s.c) for k in range(8)]
     with jax.named_scope("wait_z"):
         all_come(zbuf.at[pl.ds(1, s.nz - 1)], z_k, f, r)
         total = zbuf[0].astype(F32)
@@ -386,8 +403,6 @@
         ybuf[0, r] = ysrc[second]
 
     with jax.named_scope("wait_d"):
-        for c in c_nb:
-            c.wait_recv()
         all_come(table.at[1 - core], d_k, f, partner)
 
     with jax.named_scope("rows"):
@@ -397,15 +412,12 @@
                 held[:, (4 * half + q) * s.q : (4 * half + q + 1) * s.q] = got[q * rows : (q + 1) * rows]
         total_col = jnp.zeros((rows, 1), F32)
         total_sq = jnp.zeros((rows, 1), F32)
-        size = length[:rows]
         for j in range(chunks):
             lo, hi = j * s.sl, (j + 1) * s.sl
-            new = DECAY * held[:, lo:hi] + (1.0 - DECAY) * full_sums(gs[j], lo, hi) / size
+            new = DECAY * held[:, lo:hi] + cols[:, lo:hi]
             cols[:, lo:hi] = new
             total_col = total_col + jnp.sum(new, axis=1, keepdims=True)
             total_sq = total_sq + jnp.sum(new * new, axis=1, keepdims=True)
-        stats = full_sums(gs[chunks, :, :128], s.c, s.cw)
-        means = [(stats[:, k : k + 1] + stats[:, k + 8 : k + 9]) / (size * s.c) for k in range(8)]
         col_mean = total_col / s.c
         feats = log_features(means, col_mean, total_sq / s.c)
         for c in weights:
@@ -432,17 +444,21 @@
     blocks = rows // 16
     outs = []
 
+    with jax.named_scope("nets"):
+        made = gen[...].astype(BF16).astype(F32)
+        groups = [made[8 * i : 8 * i + 8].astype(BF16) for i in range(rows // 8)]
+        wide1 = [jnp.where(keep, jnp.dot(spread, v, preferred_element_type=F32), 0.0).astype(BF16) for v in groups]
+        for i, v in enumerate(wide1):
+            net1[i] = jnp.where(diag1, jnp.dot(v, fold, preferred_element_type=F32), 0.0).astype(BF16)
+        by_out = [jnp.dot(gen[...].astype(BF16), pick_w2[o], preferred_element_type=F32) for o in range(3)]
+        for i in range(rows // 8):
+            w2 = [jnp.where(diag2, v[8 * i : 8 * i + 8], 0.0) for v in by_out]
+            net2[i] = jnp.concatenate(w2, axis=0).astype(BF16)
+
     def block(i):
         at = 16 * i
-        made = gen[at : at + 16, :].astype(BF16).astype(F32)
         sc = scales[at : at + 16, :]
-        nets = []
-        for half in range(2):
-            mine = made[8 * half : 8 * half + 8].astype(BF16)
-            y1 = jnp.where(keep, jnp.dot(spread, mine, preferred_element_type=F32), 0.0).astype(BF16)
-            w1 = jnp.where(diag1, jnp.dot(y1, fold, preferred_element_type=F32), 0.0).astype(BF16)
-            w2 = [jnp.where(diag2, jnp.dot(mine, pick_w2[o], preferred_element_type=F32), 0.0) for o in range(3)]
-            nets.append((w1, jnp.concatenate(w2, axis=0).astype(BF16)))
+        nets = [(net1[2 * i + half], net2[2 * i + half]) for half in range(2)]
         for j in range(s.c // wide):
             lo, hi = j * wide, (j + 1) * wide
             g16 = grads[at : at + 16, lo:hi].astype(F32)
@@ -567,7 +583,8 @@
             VMEM((s.ny, s.rep, 2, s.sl), BF16),
             one(9), one(10), one(s.ny), one(8 + 2 * s.ny), one(s.ny + s.rep),
             VMEM((rows, s.c), F32), VMEM((2 * s.rep, s.cw), F32), VMEM((rows, width), F32), VMEM((rows, 128), F32),
-            VMEM((3, width, 8 * s.hm), BF16), VMEM((4, 8, s.hid), F32),
+            VMEM((3, width, 8 * s.hm), BF16), VMEM((rows // 8, 8 * s.hm, 8 * (FIN + 2)), BF16),
+            VMEM((rows // 8, 24, 8 * s.hm), BF16), VMEM((4, 8, s.hid), F32),
             VMEM((rows, 8 * s.q), F32),
         ] + [VMEM(o.shape, o.dtype) for o in outs],
         compiler_params=pltpu.CompilerParams(collective_id=0, has_side_effects=True, vmem_limit_bytes=LIMIT),

time: 43.6 us -> 42.1 us (0.966)
  Pallas kernels: 42.7 us -> 41.3 us
    pallas_call x1, Pallas kernels: 40.7 us -> 39.3 us  [on_device(): pl.pallas_call(functools.partial(kernel, s), out_shape=outs, in_specs=[AN...]
where the time goes in v3:
time: 42.1 us; the launch traced here: 42 us
  Pallas kernels  41.3 us (98%)
  between operations  0.65 us (2%)
    pallas_call x1, Pallas kernels, on_device(): pl.pallas_call(functools.partial(kernel, s), out_shape=outs, in_specs=[AN...  39.3 us
    pallas_call x1, Pallas kernels, on_device(): pl.pallas_call(put_out, out_shape=outs, in_specs=[ANY] * 5, out_specs=(AN...  2.04 us

profile of v3, /device:TPU:1, one launch (start us, length us, event | category | flops | bytes accessed | tf_op | source)
XLA Modules:
  0.0 42.0 jit_solution(14699083029298522113)
XLA Ops:
  0.6 39.3 %step.1 = (f32[48,3584]{1,0:T(8,128)}, f32[1,48]{1,0:T(1,128)}, f32[2,3584]{1,0:T(2,128)}, f32[2,512]{1,0:T(2,128)}, f32[2,512]{1,0:T(2,128)}) custom-call(f32[48,3584]{1,0:T(8,128)} %params_h.1, bf16[48,3584]{1,0:T(8,128)(2,1)} %grads_h.1, bf16[3,48,3584]{2,1,0:T(8,128)(2,1)} %moments_h.1, f32[1,48]{1,0:T(1,128)} %bitcast.6, s32[1,128]{1,0:T(1,128)} %bitcast.7, ...), custom_call_target="tpu_custom_call" | custom-call | tf_op jit(solution)/shard_map/step/pallas_call | solution.py:572
  39.9 2.0 %out.1 = (f32[48,3584]{1,0:T(8,128)}, f32[1,48]{1,0:T(1,128)}, f32[2,3584]{1,0:T(2,128)}, f32[2,512]{1,0:T(2,128)}, f32[2,512]{1,0:T(2,128)}) custom-call(f32[48,3584]{1,0:T(8,128)} %get-tuple-element.15.refs_0_, f32[1,48]{1,0:T(1,128)} %get-tuple-element.16.refs_1_, f32[2,3584]{1,0:T(2,128)} %get-tuple-element.17.refs_2_, ...), custom_call_target="tpu_custom_call" | custom-call | tf_op jit(solution)/shard_map/out/pallas_call | solution.py:593

commit v4 on v3

--- a/solution.py
+++ b/solution.py
@@ -192,7 +192,7 @@
             return c
 
         def pass_on(piece, src):
-            for k in (2, 6, 1, 7) if piece in early else near[::-1]:
+            for k in (2, 6, 1, 7) if piece in early else near:
                 t_two[k, piece] = hop(src, k, piece, k)
 
         def relay(piece):
@@ -540,7 +540,8 @@
 
 
 def put_out(*refs):
-    here, there, held, sems = refs[:5], refs[5:10], refs[10:15], refs[15]
+    sems, rows = refs[15], refs[0].shape[0]
+    here, there, held = ([v[0].at[pl.ds(i, 16)] for i in range(0, rows, 16)] + list(v[1:]) for v in (refs[:5], refs[5:10], refs[10:15]))
     come = [pltpu.make_async_copy(a, b, sems.at[0, i]) for i, (a, b) in enumerate(zip(here, held))]
     go = [pltpu.make_async_copy(a, b, sems.at[1, i]) for i, (a, b) in enumerate(zip(held, there))]
     for c in come:
@@ -595,7 +596,7 @@
         out_shape=outs,
         in_specs=[ANY] * 5,
         out_specs=(ANY,) * 5,
-        scratch_shapes=[VMEM(o.shape, o.dtype) for o in outs] + [sems(5)],
+        scratch_shapes=[VMEM(o.shape, o.dtype) for o in outs] + [sems(rows // 16 + 4)],
         compiler_params=pltpu.CompilerParams(vmem_limit_bytes=LIMIT),
         name="out",
     )(*made)

time: 42.1 us -> 42.1 us (level)
  no operation moved by 1% of the time
where the time goes in v4:
time: 42.1 us; the launch traced here: 42 us
  Pallas kernels  41.3 us (98%)
  between operations  0.65 us (2%)
    pallas_call x1, Pallas kernels, on_device(): pl.pallas_call(functools.partial(kernel, s), out_shape=outs, in_specs=[AN...  39.3 us
    pallas_call x1, Pallas kernels, on_device(): pl.pallas_call(put_out, out_shape=outs, in_specs=[ANY] * 5, out_specs=(AN...  1.98 us

profile of v4, /device:TPU:1, one launch (start us, length us, event | category | flops | bytes accessed | tf_op | source)
XLA Modules:
  0.0 42.0 jit_solution(9232992863443331800)
XLA Ops:
  0.6 39.3 %step.1 = (f32[48,3584]{1,0:T(8,128)}, f32[1,48]{1,0:T(1,128)}, f32[2,3584]{1,0:T(2,128)}, f32[2,512]{1,0:T(2,128)}, f32[2,512]{1,0:T(2,128)}) custom-call(f32[48,3584]{1,0:T(8,128)} %params_h.1, bf16[48,3584]{1,0:T(8,128)(2,1)} %grads_h.1, bf16[3,48,3584]{2,1,0:T(8,128)(2,1)} %moments_h.1, f32[1,48]{1,0:T(1,128)} %bitcast.6, s32[1,128]{1,0:T(1,128)} %bitcast.7, ...), custom_call_target="tpu_custom_call" | custom-call | tf_op jit(solution)/shard_map/step/pallas_call | solution.py:573
  40.0 2.0 %out.1 = (f32[48,3584]{1,0:T(8,128)}, f32[1,48]{1,0:T(1,128)}, f32[2,3584]{1,0:T(2,128)}, f32[2,512]{1,0:T(2,128)}, f32[2,512]{1,0:T(2,128)}) custom-call(f32[48,3584]{1,0:T(8,128)} %get-tuple-element.15.refs_0_, f32[1,48]{1,0:T(1,128)} %get-tuple-element.16.refs_1_, f32[2,3584]{1,0:T(2,128)} %get-tuple-element.17.refs_2_, ...), custom_call_target="tpu_custom_call" | custom-call | tf_op jit(solution)/shard_map/out/pallas_call | solution.py:594
